TPU v7x, 32 devices: a whole 2x2x4 slice. The times are simulated.
32 devices in a mesh: batch: 8 (over z, y), cols: 2 (over core), ens: 2 (over x).
Axes of the slice: x: 2, y: 2, z: 4, core: 2. Of those that a mesh axis runs over, the one named last changes fastest.
Arguments:
- slope_up: float32 [16, 1280, 5120], P(('ens', 'batch'), None, 'cols'), parts along dimension 0, may hold values from -0.875 to 0.875
- slope_down: float32 [16, 5120, 1280], P(('ens', 'batch'), 'cols'), parts along dimension 0, may hold values from -0.875 to 0.875
- slope_norm: float32 [16, 1280], P(('ens', 'batch')), parts along dimension 0, may hold values from -8 to 8
- slope_bias: float32 [16, 1280], P(('ens', 'batch')), parts along dimension 0, may hold values from -8 to 8
- param_up: float32 [2560, 5120], P(('ens', 'batch'), 'cols'), parts along dimension 0, may hold values from -0.25 to 0.25
- param_down: float32 [10240, 1280], P(('ens', 'cols'), 'batch'), parts along dimension 0, may hold values from -0.125 to 0.125
- param_norm: float32 [2560], P(('ens', 'batch')), parts along dimension 0, may hold values from 0.25 to 1.75
- param_bias: float32 [2560], P(('ens', 'batch')), parts along dimension 0, may hold values from -3 to 3
Outputs:
- half_up: bfloat16 [2560, 5120], P('ens', 'cols'), parts along dimension 0
- half_down: bfloat16 [10240, 1280], P(('ens', 'cols')), parts along dimension 0
- half_norm: bfloat16 [2560], P('ens'), parts along dimension 0
- half_bias: bfloat16 [2560], P('ens'), parts along dimension 0
- next_up: float32 [2560, 5120], P(('ens', 'batch'), 'cols'), parts along dimension 0
- next_down: float32 [10240, 1280], P(('ens', 'cols'), 'batch'), parts along dimension 0
- next_norm: float32 [2560], P(('ens', 'batch')), parts along dimension 0
- next_bias: float32 [2560], P(('ens', 'batch')), parts along dimension 0
There are 2 independent parts, one for each index of `ens`. A program takes and returns all parts, laid end to end along the dimension named above; each array names one. Nothing has to cross between parts.
All inputs are finite; a program needn't handle non-finite values.
Results may differ from a plain program's by a relative error of at most 0.008.
Values may be sent and summed in bfloat16 or wider, within the bound.
A program may use at most 128 MiB of HBM per device.

v0:
```python
import functools

import jax
import jax.numpy as jnp
from jax import lax
from jax.experimental import pallas as pl
from jax.experimental.pallas import tpu as pltpu
from jax.sharding import PartitionSpec as P

learn_rate = 0.4
MESH = pl.DeviceIdType.MESH
R = 8
LANE = 128
SPLIT = 0.6
F32, BF16 = jnp.float32, jnp.bfloat16


def kernel(
    n,
    m,
    LA,
    up_ref,
    down_ref,
    pup_ref,
    pdown_ref,
    vec_ref,
    half_up_ref,
    half_down_ref,
    next_up_ref,
    next_down_ref,
    sums_ref,
    stage,
    turn,
    XA,
    XB,
    RYA,
    RYB,
    RZA,
    RZB,
    NX,
    PR,
    SQ,
    GA,
    GB,
    VG,
    up_sem,
    down_sem,
    par_sem,
    out_sem,
    send,
    recv,
    sq_send,
    sq_recv,
    v_send,
    v_recv,
):
    Z = n // 2
    C = NX.shape[0]
    CH = C // 2
    L = NX.shape[2]
    me = lax.axis_index("batch")
    core = lax.axis_index("cols")
    z = me // 2
    y = me % 2
    other = z * 2 + 1 - y
    rate = n ** (-0.5)

    def load_up(c):
        return pltpu.make_async_copy(up_ref.at[:, :, c], stage.at[c % 2], up_sem.at[c % 2])

    blocks = L // LANE
    share = -(-blocks // CH)

    def load_down(b):
        return pltpu.make_async_copy(
            down_ref.at[pl.ds(b * LANE, LANE)], turn.at[b % 2], down_sem.at[b % 2]
        )

    def turn_block(b):
        def pieces(store):
            for j in range(n * CH * R // LANE):
                tile = turn[b % 2, :, j * LANE : (j + 1) * LANE].T
                for i in range(LANE // R):
                    piece = j * (LANE // R) + i
                    d, k = piece // CH, piece % CH
                    store(d // 2, d % 2, CH + k, tile[i * R : (i + 1) * R].astype(BF16))

        @pl.when(b * LANE < LA)
        def _():
            at = pl.ds(pl.multiple_of(b * LANE, LANE), LANE)

            def store(d, v, c, x):
                XA[c, v, d, :, at] = x

            pieces(store)

        @pl.when(b * LANE >= LA)
        def _():
            at = pl.ds(pl.multiple_of(b * LANE - LA, LANE), LANE)

            def store(d, v, c, x):
                XB[c, d, v, :, at] = x

            pieces(store)

    def load_params():
        return [
            pltpu.make_async_copy(pup_ref, PR.at[pl.ds(0, CH)], par_sem.at[0]),
            pltpu.make_async_copy(pdown_ref, PR.at[pl.ds(CH, CH)], par_sem.at[1]),
        ]

    load_up(0).start()
    for d in load_params():
        d.start()

    load_down(0).start()

    barrier = pltpu.get_barrier_semaphore()
    for o in range(1, n):
        pl.semaphore_signal(
            barrier, inc=1, device_id={"batch": (me + o) % n}, device_id_type=MESH
        )
    for o in range(1, m):
        pl.semaphore_signal(
            barrier, inc=1, device_id={"cols": (core + o) % m}, device_id_type=MESH
        )
    pl.semaphore_wait(barrier, n - 1 + m - 1)

    def remote(src, dst, kind, c, to):
        return pltpu.make_async_remote_copy(
            src_ref=src,
            dst_ref=dst,
            send_sem=send.at[kind, c],
            recv_sem=recv.at[kind, c],
            device_id={"batch": to},
            device_id_type=MESH,
        )

    def vec_copy(o):
        return pltpu.make_async_remote_copy(
            src_ref=vec_ref,
            dst_ref=VG.at[o - 1],
            send_sem=v_send.at[o - 1],
            recv_sem=v_recv.at[o - 1],
            device_id={"batch": (me + o) % n},
            device_id_type=MESH,
        )

    for o in range(1, n):
        vec_copy(o).start()

    def sq_copy(c, o):
        return pltpu.make_async_remote_copy(
            src_ref=SQ.at[c, 0],
            dst_ref=SQ.at[c, o],
            send_sem=sq_send.at[o - 1, c],
            recv_sem=sq_recv.at[o - 1, c],
            device_id={"cols": (core + o) % m},
            device_id_type=MESH,
        )

    YA, YB, RA, LFA, RB, LFB, GYA, GYB, GRA, GLA, GRB, GLB = range(12)

    def ya(c):
        return remote(XA.at[c, 1 - y], RYA.at[c], YA, c, other)

    def yb(c):
        return remote(XB.at[c, z, 1 - y], RYB.at[c], YB, c, other)

    def gya(c):
        return remote(GA.at[c, y], GA.at[c, y], GYA, c, other)

    def gya_in(c):
        return remote(GA.at[c, 1 - y], GA.at[c, 1 - y], GYA, c, other)

    def gyb(c):
        return remote(GB.at[c, z, y], GB.at[c, z, y], GYB, c, other)

    def gyb_in(c):
        return remote(GB.at[c, z, 1 - y], GB.at[c, z, 1 - y], GYB, c, other)

    def x_ref(first, c):
        return XA.at[c, y] if first else XB.at[c]

    def sum_right(first, c, k):
        rz = RZA if first else RZB
        return remote(
            x_ref(first, c).at[pl.ds(k + 1, Z - 1 - k)],
            rz.at[c, pl.ds(k + 2, Z - 1 - k)],
            RA if first else RB,
            c,
            jnp.minimum(me + 2, n - 1),
        )

    def sum_left(first, c, k):
        rz = RZA if first else RZB
        return remote(
            x_ref(first, c).at[pl.ds(0, k)],
            rz.at[c, pl.ds(0, k)],
            LFA if first else LFB,
            c,
            jnp.maximum(me - 2, 0),
        )

    def add(first, c, lo, count, slot):
        rz = RZA if first else RZB
        for d in range(count):
            if first:
                XA[c, y, lo + d] = (
                    XA[c, y, lo + d].astype(F32) + rz[c, slot + d].astype(F32)
                ).astype(BF16)
            else:
                XB[c, lo + d] = (
                    XB[c, lo + d].astype(F32) + rz[c, slot + d].astype(F32)
                ).astype(BF16)

    def reduce_step(first, t):
        for k in range(Z):

            @pl.when((z == k) & (t - k >= 0) & (t - k < C))
            def _():
                c = t - k
                if k > 0:
                    sum_right(first, c, k - 1).wait_recv()
                    add(first, c, k, Z - k, k + 1)
                if k < Z - 1:
                    sum_right(first, c, k).start()

            q = Z - 1 - k

            @pl.when((z == k) & (t - q >= 0) & (t - q < C))
            def _():
                c = t - q
                if k < Z - 1:
                    sum_left(first, c, k + 1).wait_recv()
                    add(first, c, 0, k + 1, 0)
                if k > 0:
                    sum_left(first, c, k).start()

    def g_ref(first, c):
        return GA.at[c, y] if first else GB.at[c]

    def gather_right(first, c, k):
        ref = g_ref(first, c).at[pl.ds(0, k + 1)]
        return remote(ref, ref, GRA if first else GRB, c, jnp.minimum(me + 2, n - 1))

    def gather_left(first, c, k):
        ref = g_ref(first, c).at[pl.ds(k, Z - k)]
        return remote(ref, ref, GLA if first else GLB, c, jnp.maximum(me - 2, 0))

    def gather_step(first, t):
        for k in range(Z):

            @pl.when((z == k) & (t - k >= 0) & (t - k < C))
            def _():
                c = t - k
                if k > 0:
                    gather_right(first, c, k - 1).wait_recv()
                if k < Z - 1:
                    gather_right(first, c, k).start()

            q = Z - 1 - k

            @pl.when((z == k) & (t - q >= 0) & (t - q < C))
            def _():
                c = t - q
                if k < Z - 1:
                    gather_left(first, c, k + 1).wait_recv()
                if k > 0:
                    gather_left(first, c, k).start()

    def outs(c, act):
        def each(half_ref, k):
            for d in (
                pltpu.make_async_copy(
                    GA.at[c, 0], half_ref.at[:, 0, k, :, pl.ds(0, LA)], out_sem.at[0, c]
                ),
                pltpu.make_async_copy(
                    GA.at[c, 1], half_ref.at[:, 1, k, :, pl.ds(0, LA)], out_sem.at[1, c]
                ),
                pltpu.make_async_copy(
                    GB.at[c], half_ref.at[:, :, k, :, pl.ds(LA, L - LA)], out_sem.at[2, c]
                ),
            ):
                act(d)

        @pl.when(c < CH)
        def _():
            each(half_up_ref, c)

        @pl.when(c >= CH)
        def _():
            each(half_down_ref, c - CH)

    def next_out(c, act):
        @pl.when(c < CH)
        def _():
            act(pltpu.make_async_copy(NX.at[c], next_up_ref.at[c], out_sem.at[3, c]))

        @pl.when(c >= CH)
        def _():
            act(pltpu.make_async_copy(NX.at[c], next_down_ref.at[c - CH], out_sem.at[3, c]))

    def lanes(x):
        s = x[:, :LANE] * x[:, :LANE]
        for i in range(1, L // LANE):
            part = x[:, i * LANE : (i + 1) * LANE]
            s = s + part * part
        return s

    def when_chunk(c):
        return pl.when((c >= 0) & (c < C))

    @pl.loop(0, C + 2 * Z)
    def _(t):
        @pl.when(t + 1 < CH)
        def _():
            load_up(t + 1).start()

        @pl.when(t < CH)
        def _():
            load_up(t).wait()
            for d in range(Z):
                for v in range(2):
                    XA[t, v, d] = stage[t % 2, d, v, :, :LA].astype(BF16)
                    XB[t, d, v] = stage[t % 2, d, v, :, LA:].astype(BF16)

        @pl.when(t < C)
        def _():
            ya(t).start()

        reduce_step(False, t)
        s = t - 1

        @when_chunk(s)
        def _():
            ya(s).wait_recv()
            for d in range(Z):
                XA[s, y, d] = (XA[s, y, d].astype(F32) + RYA[s, d].astype(F32)).astype(BF16)

        reduce_step(True, s)
        b = t - (Z - 1)

        @when_chunk(b)
        def _():
            yb(b).start()

        f = t - Z

        @pl.when(f == 0)
        def _():
            for d in load_params():
                d.wait()

        @when_chunk(f)
        def _():
            yb(f).wait_recv()
            NX[f, :, :LA] = XA[f, y, z].astype(F32) * rate
            NX[f, :, LA:] = (XB[f, z, y].astype(F32) + RYB[f].astype(F32)) * rate
            SQ[f, 0, 0] = lanes(NX[f])
            SQ[f, 0, 1] = lanes(PR[f])
            for o in range(1, m):
                sq_copy(f, o).start()

        u = t - Z

        @when_chunk(u - 1)
        def _():
            gyb_in(u - 1).wait_recv()

        gather_step(False, u - 1)
        e = u - Z

        @when_chunk(e)
        def _():
            gya_in(e).wait_recv()
            outs(e, lambda d: d.start())

        @when_chunk(u)
        def _():
            for o in range(1, m):
                sq_copy(u, o).wait_recv()
            g = SQ[u, 0, 0]
            p = SQ[u, 0, 1]
            for o in range(1, m):
                g = g + SQ[u, o, 0]
                p = p + SQ[u, o, 1]
            g = jnp.sum(g, axis=1, keepdims=True)
            p = jnp.sum(p, axis=1, keepdims=True)
            scale = learn_rate * (jnp.sqrt(p) * lax.rsqrt(g + 1e-06))
            new = PR[u] - NX[u] * scale
            NX[u] = new
            half = new.astype(BF16)
            GA[u, y, z] = half[:, :LA]
            GB[u, z, y] = half[:, LA:]
            gyb(u).start()
            next_out(u, lambda d: d.start())

        gather_step(True, u)

        @when_chunk(u - (Z - 1))
        def _():
            gya(u - (Z - 1)).start()

        for i in range(share):
            b = t * share + i

            @pl.when(b + 1 < blocks)
            def _():
                load_down(b + 1).start()

            @pl.when(b < blocks)
            def _():
                load_down(b).wait()
                turn_block(b)

    total = vec_ref[...]
    for o in range(1, n):
        vec_copy(o).wait()
        total = total + VG[o - 1]
    sums_ref[...] = total

    @pl.loop(0, C)
    def _(c):
        outs(c, lambda d: d.wait())
        next_out(c, lambda d: d.wait())
        for d in (ya(c), yb(c), gya(c), gyb(c)):
            d.wait_send()
        for o in range(1, m):
            sq_copy(c, o).wait_send()
        for k in range(Z):

            @pl.when(z == k)
            def _():
                for first in (True, False):
                    if k < Z - 1:
                        sum_right(first, c, k).wait_send()
                        gather_right(first, c, k).wait_send()
                    if k > 0:
                        sum_left(first, c, k).wait_send()
                        gather_left(first, c, k).wait_send()


def on_device(
    slope_up, slope_down, slope_norm, slope_bias, param_up, param_down, param_norm, param_bias
):
    n = lax.axis_size("batch")
    m = lax.axis_size("cols")
    Z = n // 2
    rows, L = param_up.shape
    CH = rows // R
    C = 2 * CH
    LA = max(1, round(SPLIT * L / LANE)) * LANE
    LB = L - LA
    width = slope_norm.shape[1]
    place = lax.axis_index("batch")
    up = slope_up[0].reshape(Z, 2, CH, R, L)
    down = slope_down[0]
    pup = param_up.reshape(CH, R, L)
    pdown = param_down.T.reshape(CH, R, L)
    mine = lax.dynamic_update_slice(
        jnp.zeros((2, width), F32), jnp.stack([param_norm, param_bias]), (0, place * rows)
    )
    vec = jnp.concatenate([slope_norm, slope_bias, mine], axis=0).reshape(8, width // 2)
    kinds = 12
    hbm = pl.BlockSpec(memory_space=pl.ANY)
    vmem = pl.BlockSpec(memory_space=pltpu.VMEM)
    half_up, half_down, new_up, new_down, sums = pl.pallas_call(
        functools.partial(kernel, n, m, LA),
        out_shape=(
            jax.ShapeDtypeStruct((Z, 2, CH, R, L), BF16),
            jax.ShapeDtypeStruct((Z, 2, CH, R, L), BF16),
            jax.ShapeDtypeStruct((CH, R, L), F32),
            jax.ShapeDtypeStruct((CH, R, L), F32),
            jax.ShapeDtypeStruct(vec.shape, F32),
        ),
        in_specs=[hbm, hbm, hbm, hbm, vmem],
        out_specs=(hbm, hbm, hbm, hbm, vmem),
        scratch_shapes=[
            pltpu.VMEM((2, Z, 2, R, L), F32),
            pltpu.VMEM((2, LANE, n * rows), F32),
            pltpu.VMEM((C, 2, Z, R, LA), BF16),
            pltpu.VMEM((C, Z, 2, R, LB), BF16),
            pltpu.VMEM((C, Z, R, LA), BF16),
            pltpu.VMEM((C, R, LB), BF16),
            pltpu.VMEM((C, Z + 1, R, LA), BF16),
            pltpu.VMEM((C, Z + 1, 2, R, LB), BF16),
            pltpu.VMEM((C, R, L), F32),
            pltpu.VMEM((C, R, L), F32),
            pltpu.VMEM((C, m, 2, R, LANE), F32),
            pltpu.VMEM((C, 2, Z, R, LA), BF16),
            pltpu.VMEM((C, Z, 2, R, LB), BF16),
            pltpu.VMEM((n - 1,) + vec.shape, F32),
            pltpu.SemaphoreType.DMA((2,)),
            pltpu.SemaphoreType.DMA((2,)),
            pltpu.SemaphoreType.DMA((2,)),
            pltpu.SemaphoreType.DMA((4, C)),
            pltpu.SemaphoreType.DMA((kinds, C)),
            pltpu.SemaphoreType.DMA((kinds, C)),
            pltpu.SemaphoreType.DMA((m - 1, C)),
            pltpu.SemaphoreType.DMA((m - 1, C)),
            pltpu.SemaphoreType.DMA((n - 1,)),
            pltpu.SemaphoreType.DMA((n - 1,)),
        ],
        compiler_params=pltpu.CompilerParams(
            collective_id=0, has_side_effects=True, vmem_limit_bytes=67043328
        ),
    )(up, down, pup, pdown, vec)
    half_up = half_up.reshape(n * rows, L)
    half_down = half_down.reshape(n * rows, L).T
    next_up = new_up.reshape(rows, L)
    next_down = new_down.reshape(rows, L).T
    sums = sums.reshape(4, width)
    whole = sums[2:] - learn_rate * (sums[:2] * n ** (-0.5))
    own = lax.dynamic_slice_in_dim(whole, place * rows, rows, axis=1)
    halves = whole.astype(BF16)
    return (half_up, half_down, halves[0], halves[1], next_up, next_down, own[0], own[1])


def solution(mesh):
    return jax.shard_map(
        on_device,
        mesh=mesh,
        in_specs=(
            P(("ens", "batch"), None, "cols"),
            P(("ens", "batch"), "cols", None),
            P(("ens", "batch"), None),
            P(("ens", "batch"), None),
            P(("ens", "batch"), "cols"),
            P(("ens", "cols"), "batch"),
            P(("ens", "batch")),
            P(("ens", "batch")),
        ),
        out_specs=(
            P("ens", "cols"),
            P(("ens", "cols"), None),
            P("ens"),
            P("ens"),
            P(("ens", "batch"), "cols"),
            P(("ens", "cols"), "batch"),
            P(("ens", "batch")),
            P(("ens", "batch")),
        ),
        check_vma=False,
    )
```

profile of v0, /device:TPU:0, one launch (start us, length us, event | category | flops | bytes accessed | tf_op | source)
XLA Modules:
  0.0 266.8 jit_solution(11690720012033683737)
XLA Ops:
  0.6 0.7 pad_maximum_fusion.1
  1.4 0.2 dynamic_update_slice.3
  1.5 0.7 pad_maximum_fusion
  2.3 0.6 reshape.45.vec_ref
  2.9 243.8 %shard_map.143 = (bf16[4,2,20,8,2560]{4,3,2,1,0:T(8,128)(2,1)}, bf16[4,2,20,8,2560]{4,3,2,1,0:T(8,128)(2,1)}, f32[20,8,2560]{2,1,0:T(8,128)}, f32[20,8,2560]{2,1,0:T(8,128)}, f32[8,640]{1,0:T(8,128)}) custom-call(f32[4,2,20,8,2560]{4,3,2,1,0:T(8,128)} %bitcast.17, f32[2560,1280]{1,0:T(8,128)} %bitcast.18, f32[20,8,2560]{2,1,0:T(8,128)} %bitcast.24, ...), custom_call_target="tpu_custom_call" | custom-call | tf_op jit(solution)/shard_map/pallas_call | solution.py:468
  246.7 0.8 multiply_subtract_fusion
  247.5 0.6 fusion
  248.1 0.6 slice_reduce_fusion
  248.8 9.5 %copy.16 = bf16[1280,2560]{0,1:T(8,128)(2,1)} copy(bf16[1280,2560]{1,0:T(8,128)(2,1)} %bitcast.20) | data formatting | bytes 13107200 | tf_op jit(solution)/shard_map/reshape | solution.py:510
  258.2 0.0 copy-start.1
  258.2 0.0 copy-start
  258.2 6.2 %copy.21 = bf16[1280,2560]{1,0:T(8,128)(2,1)} copy(bf16[1280,2560]{1,0:T(8,128)(2,1)} %bitcast.19) | data formatting | bytes 13107200
  264.5 0.0 copy-done.1
  264.5 1.2 copy.22
  265.6 0.0 copy-done
  265.6 1.2 copy.23
  (3 shorter events, 0.0 us)
Async XLA Ops:
  258.2 6.2 %copy-start.1 = (f32[20,8,2560]{2,1,0:T(8,128)S(1)}, f32[20,8,2560]{2,1,0:T(8,128)}, u32[]{:S(2)}) copy-start(f32[20,8,2560]{2,1,0:T(8,128)} %get-tuple-element.16) | copy-start | bytes 4915204
  258.2 7.4 %copy-start = (f32[20,8,2560]{2,1,0:T(8,128)S(1)}, f32[20,8,2560]{2,1,0:T(8,128)}, u32[]{:S(2)}) copy-start(f32[20,8,2560]{2,1,0:T(8,128)} %get-tuple-element.17) | copy-start | bytes 4915204
where the time goes:
time: 267 us
  Pallas kernels  244 us (91%)
  local copies, waits for them, and re-layouts  20.1 us (8%)
    pallas_call x1, Pallas kernels, on_device(): pl.pallas_call(functools.partial(kernel, n, m, LA), out_shape=(jax.ShapeD...  244 us
    reshape x1, local copies, waits for them, and re-layouts, on_device(): half_down = half_down.reshape(n * rows, L).T  9.48 us
    unnamed x7, local copies, waits for them, and re-layouts  8.56 us

commit v1 on v0

--- a/solution.py
+++ b/solution.py
@@ -1,4 +1,5 @@
 import functools
+import math
 
 import jax
 import jax.numpy as jnp
@@ -12,6 +13,7 @@
 R = 8
 LANE = 128
 SPLIT = 0.6
+VMEM_BYTES = 66_000_000
 F32, BF16 = jnp.float32, jnp.bfloat16
 
 
@@ -24,10 +26,9 @@
     pup_ref,
     pdown_ref,
     vec_ref,
-    half_up_ref,
-    half_down_ref,
-    next_up_ref,
-    next_down_ref,
+    G,
+    T,
+    NX,
     sums_ref,
     stage,
     turn,
@@ -37,16 +38,13 @@
     RYB,
     RZA,
     RZB,
-    NX,
     PR,
     SQ,
-    GA,
-    GB,
-    VG,
+    VY,
+    VZ,
     up_sem,
     down_sem,
     par_sem,
-    out_sem,
     send,
     recv,
     sq_send,
@@ -57,6 +55,7 @@
     Z = n // 2
     C = NX.shape[0]
     CH = C // 2
+    H0 = CH // 2
     L = NX.shape[2]
     me = lax.axis_index("batch")
     core = lax.axis_index("cols")
@@ -65,11 +64,15 @@
     other = z * 2 + 1 - y
     rate = n ** (-0.5)
 
+    def slot(p):
+        return jnp.where(p < H0, p, jnp.where(p < H0 + CH, p - H0 + CH, p - CH))
+
     def load_up(c):
         return pltpu.make_async_copy(up_ref.at[:, :, c], stage.at[c % 2], up_sem.at[c % 2])
 
     blocks = L // LANE
-    share = -(-blocks // CH)
+    share = -(-blocks // H0)
+    back = -(-blocks // (CH - H0))
 
     def load_down(b):
         return pltpu.make_async_copy(
@@ -136,18 +139,25 @@
             device_id_type=MESH,
         )
 
-    def vec_copy(o):
+    vec_y = pltpu.make_async_remote_copy(
+        src_ref=vec_ref,
+        dst_ref=VY,
+        send_sem=v_send.at[0],
+        recv_sem=v_recv.at[0],
+        device_id={"batch": other},
+        device_id_type=MESH,
+    )
+    vec_y.start()
+
+    def vec_z(o):
         return pltpu.make_async_remote_copy(
-            src_ref=vec_ref,
-            dst_ref=VG.at[o - 1],
-            send_sem=v_send.at[o - 1],
-            recv_sem=v_recv.at[o - 1],
-            device_id={"batch": (me + o) % n},
+            src_ref=VZ.at[z],
+            dst_ref=VZ.at[z],
+            send_sem=v_send.at[o],
+            recv_sem=v_recv.at[o],
+            device_id={"batch": (me + 2 * o) % n},
             device_id_type=MESH,
         )
-
-    for o in range(1, n):
-        vec_copy(o).start()
 
     def sq_copy(c, o):
         return pltpu.make_async_remote_copy(
@@ -168,16 +178,20 @@
         return remote(XB.at[c, z, 1 - y], RYB.at[c], YB, c, other)
 
     def gya(c):
-        return remote(GA.at[c, y], GA.at[c, y], GYA, c, other)
+        ref = G.at[:, y, c, :, pl.ds(0, LA)]
+        return remote(ref, ref, GYA, c, other)
 
     def gya_in(c):
-        return remote(GA.at[c, 1 - y], GA.at[c, 1 - y], GYA, c, other)
+        ref = G.at[:, 1 - y, c, :, pl.ds(0, LA)]
+        return remote(ref, ref, GYA, c, other)
 
     def gyb(c):
-        return remote(GB.at[c, z, y], GB.at[c, z, y], GYB, c, other)
+        ref = G.at[z, y, c, :, pl.ds(LA, L - LA)]
+        return remote(ref, ref, GYB, c, other)
 
     def gyb_in(c):
-        return remote(GB.at[c, z, 1 - y], GB.at[c, z, 1 - y], GYB, c, other)
+        ref = G.at[z, 1 - y, c, :, pl.ds(LA, L - LA)]
+        return remote(ref, ref, GYB, c, other)
 
     def x_ref(first, c):
         return XA.at[c, y] if first else XB.at[c]
@@ -219,7 +233,7 @@
 
             @pl.when((z == k) & (t - k >= 0) & (t - k < C))
             def _():
-                c = t - k
+                c = slot(t - k)
                 if k > 0:
                     sum_right(first, c, k - 1).wait_recv()
                     add(first, c, k, Z - k, k + 1)
@@ -230,22 +244,25 @@
 
             @pl.when((z == k) & (t - q >= 0) & (t - q < C))
             def _():
-                c = t - q
+                c = slot(t - q)
                 if k < Z - 1:
                     sum_left(first, c, k + 1).wait_recv()
                     add(first, c, 0, k + 1, 0)
                 if k > 0:
                     sum_left(first, c, k).start()
 
-    def g_ref(first, c):
-        return GA.at[c, y] if first else GB.at[c]
+    def g_ref(first, c, lo, count):
+        at = pl.ds(lo, count)
+        if first:
+            return G.at[at, y, c, :, pl.ds(0, LA)]
+        return G.at[at, :, c, :, pl.ds(LA, L - LA)]
 
     def gather_right(first, c, k):
-        ref = g_ref(first, c).at[pl.ds(0, k + 1)]
+        ref = g_ref(first, c, 0, k + 1)
         return remote(ref, ref, GRA if first else GRB, c, jnp.minimum(me + 2, n - 1))
 
     def gather_left(first, c, k):
-        ref = g_ref(first, c).at[pl.ds(k, Z - k)]
+        ref = g_ref(first, c, k, Z - k)
         return remote(ref, ref, GLA if first else GLB, c, jnp.maximum(me - 2, 0))
 
     def gather_step(first, t):
@@ -253,7 +270,7 @@
 
             @pl.when((z == k) & (t - k >= 0) & (t - k < C))
             def _():
-                c = t - k
+                c = slot(t - k)
                 if k > 0:
                     gather_right(first, c, k - 1).wait_recv()
                 if k < Z - 1:
@@ -263,43 +280,22 @@
 
             @pl.when((z == k) & (t - q >= 0) & (t - q < C))
             def _():
-                c = t - q
+                c = slot(t - q)
                 if k < Z - 1:
                     gather_left(first, c, k + 1).wait_recv()
                 if k > 0:
                     gather_left(first, c, k).start()
 
-    def outs(c, act):
-        def each(half_ref, k):
-            for d in (
-                pltpu.make_async_copy(
-                    GA.at[c, 0], half_ref.at[:, 0, k, :, pl.ds(0, LA)], out_sem.at[0, c]
-                ),
-                pltpu.make_async_copy(
-                    GA.at[c, 1], half_ref.at[:, 1, k, :, pl.ds(0, LA)], out_sem.at[1, c]
-                ),
-                pltpu.make_async_copy(
-                    GB.at[c], half_ref.at[:, :, k, :, pl.ds(LA, L - LA)], out_sem.at[2, c]
-                ),
-            ):
-                act(d)
-
-        @pl.when(c < CH)
-        def _():
-            each(half_up_ref, c)
-
-        @pl.when(c >= CH)
-        def _():
-            each(half_down_ref, c - CH)
-
-    def next_out(c, act):
-        @pl.when(c < CH)
-        def _():
-            act(pltpu.make_async_copy(NX.at[c], next_up_ref.at[c], out_sem.at[3, c]))
-
-        @pl.when(c >= CH)
-        def _():
-            act(pltpu.make_async_copy(NX.at[c], next_down_ref.at[c - CH], out_sem.at[3, c]))
+    def back_block(b):
+        at = pl.ds(pl.multiple_of(b * LANE, LANE), LANE)
+        for j in range(n * CH * R // LANE):
+            rows = []
+            for i in range(LANE // R):
+                piece = j * (LANE // R) + i
+                d, k = piece // CH, piece % CH
+                rows.append(G[d // 2, d % 2, CH + k, :, at].astype(F32))
+            tile = jnp.concatenate(rows, axis=0)
+            T[at, j * LANE : (j + 1) * LANE] = tile.T.astype(BF16)
 
     def lanes(x):
         s = x[:, :LANE] * x[:, :LANE]
@@ -313,47 +309,60 @@
 
     @pl.loop(0, C + 2 * Z)
     def _(t):
-        @pl.when(t + 1 < CH)
-        def _():
-            load_up(t + 1).start()
-
-        @pl.when(t < CH)
-        def _():
-            load_up(t).wait()
+        def load_at(p, act):
+            @pl.when((p < H0) | ((p >= H0 + CH) & (p < C)))
+            def _():
+                act(slot(p))
+
+        load_at(t + 1, lambda c: load_up(c).start())
+
+        def cast(c):
+            load_up(c).wait()
             for d in range(Z):
                 for v in range(2):
-                    XA[t, v, d] = stage[t % 2, d, v, :, :LA].astype(BF16)
-                    XB[t, d, v] = stage[t % 2, d, v, :, LA:].astype(BF16)
+                    XA[c, v, d] = stage[c % 2, d, v, :, :LA].astype(BF16)
+                    XB[c, d, v] = stage[c % 2, d, v, :, LA:].astype(BF16)
+
+        load_at(t, cast)
 
         @pl.when(t < C)
         def _():
-            ya(t).start()
+            ya(slot(t)).start()
 
         reduce_step(False, t)
         s = t - 1
 
+        @pl.when(t == 1)
+        def _():
+            vec_y.wait()
+            VZ[z] = vec_ref[...] + VY[...]
+            for o in range(1, Z):
+                vec_z(o).start()
+
         @when_chunk(s)
         def _():
-            ya(s).wait_recv()
+            c = slot(s)
+            ya(c).wait_recv()
             for d in range(Z):
-                XA[s, y, d] = (XA[s, y, d].astype(F32) + RYA[s, d].astype(F32)).astype(BF16)
+                XA[c, y, d] = (XA[c, y, d].astype(F32) + RYA[c, d].astype(F32)).astype(BF16)
 
         reduce_step(True, s)
         b = t - (Z - 1)
 
         @when_chunk(b)
         def _():
-            yb(b).start()
-
-        f = t - Z
-
-        @pl.when(f == 0)
+            yb(slot(b)).start()
+
+        u = t - Z
+
+        @pl.when(u == 0)
         def _():
             for d in load_params():
                 d.wait()
 
-        @when_chunk(f)
-        def _():
+        @when_chunk(u)
+        def _():
+            f = slot(u)
             yb(f).wait_recv()
             NX[f, :, :LA] = XA[f, y, z].astype(F32) * rate
             NX[f, :, LA:] = (XB[f, z, y].astype(F32) + RYB[f].astype(F32)) * rate
@@ -362,45 +371,40 @@
             for o in range(1, m):
                 sq_copy(f, o).start()
 
-        u = t - Z
-
         @when_chunk(u - 1)
         def _():
-            gyb_in(u - 1).wait_recv()
+            gyb_in(slot(u - 1)).wait_recv()
 
         gather_step(False, u - 1)
         e = u - Z
 
         @when_chunk(e)
         def _():
-            gya_in(e).wait_recv()
-            outs(e, lambda d: d.start())
+            gya_in(slot(e)).wait_recv()
 
         @when_chunk(u)
         def _():
+            f = slot(u)
             for o in range(1, m):
-                sq_copy(u, o).wait_recv()
-            g = SQ[u, 0, 0]
-            p = SQ[u, 0, 1]
+                sq_copy(f, o).wait_recv()
+            g = SQ[f, 0, 0]
+            p = SQ[f, 0, 1]
             for o in range(1, m):
-                g = g + SQ[u, o, 0]
-                p = p + SQ[u, o, 1]
+                g = g + SQ[f, o, 0]
+                p = p + SQ[f, o, 1]
             g = jnp.sum(g, axis=1, keepdims=True)
             p = jnp.sum(p, axis=1, keepdims=True)
             scale = learn_rate * (jnp.sqrt(p) * lax.rsqrt(g + 1e-06))
-            new = PR[u] - NX[u] * scale
-            NX[u] = new
-            half = new.astype(BF16)
-            GA[u, y, z] = half[:, :LA]
-            GB[u, z, y] = half[:, LA:]
-            gyb(u).start()
-            next_out(u, lambda d: d.start())
+            new = PR[f] - NX[f] * scale
+            NX[f] = new
+            G[z, y, f] = new.astype(BF16)
+            gyb(f).start()
 
         gather_step(True, u)
 
         @when_chunk(u - (Z - 1))
         def _():
-            gya(u - (Z - 1)).start()
+            gya(slot(u - (Z - 1))).start()
 
         for i in range(share):
             b = t * share + i
@@ -414,16 +418,22 @@
                 load_down(b).wait()
                 turn_block(b)
 
-    total = vec_ref[...]
-    for o in range(1, n):
-        vec_copy(o).wait()
-        total = total + VG[o - 1]
+        for i in range(back):
+            w = (t - (H0 + CH + 2 * Z)) * back + i
+
+            @pl.when((w >= 0) & (w < blocks))
+            def _():
+                back_block(w)
+
+    for o in range(1, Z):
+        vec_z(o).wait()
+    total = VZ[0]
+    for k in range(1, Z):
+        total = total + VZ[k]
     sums_ref[...] = total
 
     @pl.loop(0, C)
     def _(c):
-        outs(c, lambda d: d.wait())
-        next_out(c, lambda d: d.wait())
         for d in (ya(c), yb(c), gya(c), gyb(c)):
             d.wait_send()
         for o in range(1, m):
@@ -439,6 +449,28 @@
                     if k > 0:
                         sum_left(first, c, k).wait_send()
                         gather_left(first, c, k).wait_send()
+
+
+def put_kernel(G, T, NX, half_up_ref, half_down_ref, next_up_ref, next_down_ref, sem):
+    Z = G.shape[0]
+    CH = G.shape[2] // 2
+    part = T.shape[0] // (2 * Z)
+    copies = []
+
+    def put(src, dst):
+        d = pltpu.make_async_copy(src, dst, sem.at[len(copies)])
+        d.start()
+        copies.append(d)
+
+    for k in range(Z):
+        for v in range(2):
+            put(G.at[k, v, pl.ds(0, CH)], half_up_ref.at[k, v])
+            at = pl.ds((2 * k + v) * part, part)
+            put(T.at[at], half_down_ref.at[at])
+    put(NX.at[pl.ds(0, CH)], next_up_ref)
+    put(NX.at[pl.ds(CH, CH)], next_down_ref)
+    for d in copies:
+        d.wait()
 
 
 def on_device(
@@ -465,17 +497,14 @@
     kinds = 12
     hbm = pl.BlockSpec(memory_space=pl.ANY)
     vmem = pl.BlockSpec(memory_space=pltpu.VMEM)
-    half_up, half_down, new_up, new_down, sums = pl.pallas_call(
+    kept = [((Z, 2, C, R, L), BF16), ((L, n * rows), BF16), ((C, R, L), F32)]
+    size = sum(jnp.dtype(dtype).itemsize * math.prod(shape) for shape, dtype in kept)
+    G, T, NX, sums = pl.pallas_call(
         functools.partial(kernel, n, m, LA),
-        out_shape=(
-            jax.ShapeDtypeStruct((Z, 2, CH, R, L), BF16),
-            jax.ShapeDtypeStruct((Z, 2, CH, R, L), BF16),
-            jax.ShapeDtypeStruct((CH, R, L), F32),
-            jax.ShapeDtypeStruct((CH, R, L), F32),
-            jax.ShapeDtypeStruct(vec.shape, F32),
-        ),
+        out_shape=tuple(pltpu.VMEM(shape, dtype) for shape, dtype in kept)
+        + (jax.ShapeDtypeStruct(vec.shape, F32),),
         in_specs=[hbm, hbm, hbm, hbm, vmem],
-        out_specs=(hbm, hbm, hbm, hbm, vmem),
+        out_specs=(vmem, vmem, vmem, vmem),
         scratch_shapes=[
             pltpu.VMEM((2, Z, 2, R, L), F32),
             pltpu.VMEM((2, LANE, n * rows), F32),
@@ -486,28 +515,37 @@
             pltpu.VMEM((C, Z + 1, R, LA), BF16),
             pltpu.VMEM((C, Z + 1, 2, R, LB), BF16),
             pltpu.VMEM((C, R, L), F32),
-            pltpu.VMEM((C, R, L), F32),
             pltpu.VMEM((C, m, 2, R, LANE), F32),
-            pltpu.VMEM((C, 2, Z, R, LA), BF16),
-            pltpu.VMEM((C, Z, 2, R, LB), BF16),
-            pltpu.VMEM((n - 1,) + vec.shape, F32),
+            pltpu.VMEM(vec.shape, F32),
+            pltpu.VMEM((Z,) + vec.shape, F32),
             pltpu.SemaphoreType.DMA((2,)),
             pltpu.SemaphoreType.DMA((2,)),
             pltpu.SemaphoreType.DMA((2,)),
-            pltpu.SemaphoreType.DMA((4, C)),
             pltpu.SemaphoreType.DMA((kinds, C)),
             pltpu.SemaphoreType.DMA((kinds, C)),
             pltpu.SemaphoreType.DMA((m - 1, C)),
             pltpu.SemaphoreType.DMA((m - 1, C)),
-            pltpu.SemaphoreType.DMA((n - 1,)),
-            pltpu.SemaphoreType.DMA((n - 1,)),
+            pltpu.SemaphoreType.DMA((Z,)),
+            pltpu.SemaphoreType.DMA((Z,)),
         ],
         compiler_params=pltpu.CompilerParams(
-            collective_id=0, has_side_effects=True, vmem_limit_bytes=67043328
+            collective_id=0, has_side_effects=True, vmem_limit_bytes=VMEM_BYTES - size
         ),
     )(up, down, pup, pdown, vec)
+    half_up, half_down, new_up, new_down = pl.pallas_call(
+        put_kernel,
+        out_shape=(
+            jax.ShapeDtypeStruct((Z, 2, CH, R, L), BF16),
+            jax.ShapeDtypeStruct((L, n * rows), BF16),
+            jax.ShapeDtypeStruct((CH, R, L), F32),
+            jax.ShapeDtypeStruct((CH, R, L), F32),
+        ),
+        in_specs=[vmem] * 3,
+        out_specs=(hbm,) * 4,
+        scratch_shapes=[pltpu.SemaphoreType.DMA((4 * Z + 2,))],
+        compiler_params=pltpu.CompilerParams(vmem_limit_bytes=1 << 20),
+    )(*(pltpu.with_memory_space_constraint(x, pltpu.VMEM) for x in (G, T, NX)))
     half_up = half_up.reshape(n * rows, L)
-    half_down = half_down.reshape(n * rows, L).T
     next_up = new_up.reshape(rows, L)
     next_down = new_down.reshape(rows, L).T
     sums = sums.reshape(4, width)

time: 267 us -> 252 us (0.944)
  local copies, waits for them, and re-layouts: 20.1 us -> 2.09 us
  Pallas kernels: 244 us -> 247 us
    reshape x1 -> x0, local copies, waits for them, and re-layouts: 9.48 us -> none  [on_device(): half_down = half_down.reshape(n * rows, L).T]
    unnamed x7 -> x2, local copies, waits for them, and re-layouts: 8.56 us -> 0.01 us
    pallas_call x1 -> x2, Pallas kernels: 244 us -> 247 us  [the longest x1 241 us: on_device(): pl.pallas_call(functools.partial(kernel, n, m, LA), out_shape=tuple((pltp...]
where the time goes in v1:
time: 252 us; the launch traced here: 251 us
  Pallas kernels  247 us (98%)
    pallas_call x1, Pallas kernels, on_device(): pl.pallas_call(functools.partial(kernel, n, m, LA), out_shape=tuple((pltp...  241 us
    pallas_call x1, Pallas kernels, on_device(): pl.pallas_call(put_kernel, out_shape=(jax.ShapeDtypeStruct((Z, 2, CH, R,...  5.9 us

profile of v1, /device:TPU:0, one launch (start us, length us, event | category | flops | bytes accessed | tf_op | source)
XLA Modules:
  0.0 251.3 jit_solution(14101457549942317627)
XLA Ops:
  0.6 0.7 pad_maximum_fusion.1
  1.4 0.2 dynamic_update_slice.3
  1.5 0.7 pad_maximum_fusion
  2.3 0.6 reshape.42.vec_ref
  2.9 241.2 %shard_map.143 = (bf16[4,2,40,8,2560]{4,3,2,1,0:T(8,128)(2,1)S(1)}, bf16[2560,1280]{1,0:T(8,128)(2,1)S(1)}, f32[40,8,2560]{2,1,0:T(8,128)S(1)}, f32[8,640]{1,0:T(8,128)}) custom-call(f32[4,2,20,8,2560]{4,3,2,1,0:T(8,128)} %bitcast.15, f32[2560,1280]{1,0:T(8,128)} %bitcast.16, f32[20,8,2560]{2,1,0:T(8,128)} %bitcast.17, f32[20,8,2560]{2,1,0:T(8,128)} %bitcast.18, ...), custom_call_target="tpu_custom_call" | custom-call | tf_op jit(solution)/shard_map/pallas_call | solution.py:502
  244.1 0.0 copy-start
  244.1 5.9 %shard_map.144 = (bf16[4,2,20,8,2560]{4,3,2,1,0:T(8,128)(2,1)}, bf16[2560,1280]{1,0:T(8,128)(2,1)}, f32[20,8,2560]{2,1,0:T(8,128)}, f32[20,8,2560]{2,1,0:T(8,128)}) custom-call(bf16[4,2,40,8,2560]{4,3,2,1,0:T(8,128)(2,1)S(1)} %get-tuple-element.16.G, bf16[2560,1280]{1,0:T(8,128)(2,1)S(1)} %get-tuple-element.17.T, f32[40,8,2560]{2,1,0:T(8,128)S(1)} %get-tuple-element.18.NX), custom_call_target="tpu_custom_call" | custom-call | tf_op jit(solution)/shard_map/pallas_call | solution.py:535
  250.0 0.0 copy-done
  250.0 0.6 fusion
  250.7 0.6 slice_reduce_fusion
  (4 shorter events, 0.0 us)
Async XLA Ops:
  244.1 5.9 %copy-start = (f32[8,640]{1,0:T(8,128)S(1)}, f32[8,640]{1,0:T(8,128)}, u32[]{:S(2)}) copy-start(f32[8,640]{1,0:T(8,128)} %get-tuple-element.21) | copy-start | bytes 61444

commit v2 on v1

--- a/solution.py
+++ b/solution.py
@@ -25,7 +25,10 @@
     down_ref,
     pup_ref,
     pdown_ref,
-    vec_ref,
+    norm_ref,
+    bias_ref,
+    pnorm_ref,
+    pbias_ref,
     G,
     T,
     NX,
@@ -40,6 +43,8 @@
     RZB,
     PR,
     SQ,
+    V,
+    VP,
     VY,
     VZ,
     up_sem,
@@ -112,8 +117,16 @@
             pltpu.make_async_copy(pdown_ref, PR.at[pl.ds(CH, CH)], par_sem.at[1]),
         ]
 
+    def load_vectors():
+        return [
+            pltpu.make_async_copy(norm_ref, V.at[0], par_sem.at[2]),
+            pltpu.make_async_copy(bias_ref, V.at[1], par_sem.at[3]),
+            pltpu.make_async_copy(pnorm_ref, VP.at[0], par_sem.at[4]),
+            pltpu.make_async_copy(pbias_ref, VP.at[1], par_sem.at[5]),
+        ]
+
     load_up(0).start()
-    for d in load_params():
+    for d in load_params() + load_vectors():
         d.start()
 
     load_down(0).start()
@@ -139,15 +152,15 @@
             device_id_type=MESH,
         )
 
-    vec_y = pltpu.make_async_remote_copy(
-        src_ref=vec_ref,
-        dst_ref=VY,
-        send_sem=v_send.at[0],
-        recv_sem=v_recv.at[0],
-        device_id={"batch": other},
-        device_id_type=MESH,
-    )
-    vec_y.start()
+    def vec_y():
+        return pltpu.make_async_remote_copy(
+            src_ref=VZ.at[z],
+            dst_ref=VY,
+            send_sem=v_send.at[0],
+            recv_sem=v_recv.at[0],
+            device_id={"batch": other},
+            device_id_type=MESH,
+        )
 
     def vec_z(o):
         return pltpu.make_async_remote_copy(
@@ -332,10 +345,22 @@
         reduce_step(False, t)
         s = t - 1
 
+        @pl.when(t == 0)
+        def _():
+            for d in load_vectors():
+                d.wait()
+            width = VY.shape[1]
+            place = jnp.zeros((1, width - VP.shape[2]), F32)
+            for i in range(2):
+                VZ[z, i : i + 1] = V[i]
+                own = jnp.concatenate([VP[i], place], axis=1)
+                VZ[z, 2 + i : 3 + i] = pltpu.roll(own, me * VP.shape[2], 1)
+            vec_y().start()
+
         @pl.when(t == 1)
         def _():
-            vec_y.wait()
-            VZ[z] = vec_ref[...] + VY[...]
+            vec_y().wait()
+            VZ[z] = VZ[z] + VY[...]
             for o in range(1, Z):
                 vec_z(o).start()
 
@@ -377,10 +402,6 @@
 
         gather_step(False, u - 1)
         e = u - Z
-
-        @when_chunk(e)
-        def _():
-            gya_in(slot(e)).wait_recv()
 
         @when_chunk(u)
         def _():
@@ -406,6 +427,10 @@
         def _():
             gya(slot(u - (Z - 1))).start()
 
+        @when_chunk(e)
+        def _():
+            gya_in(slot(e)).wait_recv()
+
         for i in range(share):
             b = t * share + i
 
@@ -451,7 +476,25 @@
                         gather_left(first, c, k).wait_send()
 
 
-def put_kernel(G, T, NX, half_up_ref, half_down_ref, next_up_ref, next_down_ref, sem):
+def put_kernel(
+    G,
+    T,
+    NX,
+    sums,
+    half_up_ref,
+    half_down_ref,
+    half_norm_ref,
+    half_bias_ref,
+    next_up_ref,
+    next_down_ref,
+    next_norm_ref,
+    next_bias_ref,
+    sem,
+):
+    n = lax.axis_size("batch")
+    me = lax.axis_index("batch")
+    width = sums.shape[1]
+    rows = width // n
     Z = G.shape[0]
     CH = G.shape[2] // 2
     part = T.shape[0] // (2 * Z)
@@ -469,6 +512,13 @@
             put(T.at[at], half_down_ref.at[at])
     put(NX.at[pl.ds(0, CH)], next_up_ref)
     put(NX.at[pl.ds(CH, CH)], next_down_ref)
+    whole = sums[2:4] - learn_rate * (sums[0:2] * n ** (-0.5))
+    halves = whole.astype(BF16)
+    half_norm_ref[...] = halves[0:1].reshape(width)
+    half_bias_ref[...] = halves[1:2].reshape(width)
+    own = pltpu.roll(whole, (n - me) % n * rows, 1)[:, :rows]
+    next_norm_ref[...] = own[0:1].reshape(rows)
+    next_bias_ref[...] = own[1:2].reshape(rows)
     for d in copies:
         d.wait()
 
@@ -485,26 +535,22 @@
     LA = max(1, round(SPLIT * L / LANE)) * LANE
     LB = L - LA
     width = slope_norm.shape[1]
-    place = lax.axis_index("batch")
     up = slope_up[0].reshape(Z, 2, CH, R, L)
     down = slope_down[0]
     pup = param_up.reshape(CH, R, L)
     pdown = param_down.T.reshape(CH, R, L)
-    mine = lax.dynamic_update_slice(
-        jnp.zeros((2, width), F32), jnp.stack([param_norm, param_bias]), (0, place * rows)
-    )
-    vec = jnp.concatenate([slope_norm, slope_bias, mine], axis=0).reshape(8, width // 2)
+    pnorm = param_norm.reshape(1, rows)
+    pbias = param_bias.reshape(1, rows)
     kinds = 12
     hbm = pl.BlockSpec(memory_space=pl.ANY)
     vmem = pl.BlockSpec(memory_space=pltpu.VMEM)
-    kept = [((Z, 2, C, R, L), BF16), ((L, n * rows), BF16), ((C, R, L), F32)]
+    kept = [((Z, 2, C, R, L), BF16), ((L, n * rows), BF16), ((C, R, L), F32), ((4, width), F32)]
     size = sum(jnp.dtype(dtype).itemsize * math.prod(shape) for shape, dtype in kept)
     G, T, NX, sums = pl.pallas_call(
         functools.partial(kernel, n, m, LA),
-        out_shape=tuple(pltpu.VMEM(shape, dtype) for shape, dtype in kept)
-        + (jax.ShapeDtypeStruct(vec.shape, F32),),
-        in_specs=[hbm, hbm, hbm, hbm, vmem],
-        out_specs=(vmem, vmem, vmem, vmem),
+        out_shape=tuple(pltpu.VMEM(shape, dtype) for shape, dtype in kept),
+        in_specs=[hbm] * 8,
+        out_specs=(vmem,) * 4,
         scratch_shapes=[
             pltpu.VMEM((2, Z, 2, R, L), F32),
             pltpu.VMEM((2, LANE, n * rows), F32),
@@ -516,11 +562,13 @@
             pltpu.VMEM((C, Z + 1, 2, R, LB), BF16),
             pltpu.VMEM((C, R, L), F32),
             pltpu.VMEM((C, m, 2, R, LANE), F32),
-            pltpu.VMEM(vec.shape, F32),
-            pltpu.VMEM((Z,) + vec.shape, F32),
+            pltpu.VMEM((2, 1, width), F32),
+            pltpu.VMEM((2, 1, rows), F32),
+            pltpu.VMEM((4, width), F32),
+            pltpu.VMEM((Z, 4, width), F32),
             pltpu.SemaphoreType.DMA((2,)),
             pltpu.SemaphoreType.DMA((2,)),
-            pltpu.SemaphoreType.DMA((2,)),
+            pltpu.SemaphoreType.DMA((6,)),
             pltpu.SemaphoreType.DMA((kinds, C)),
             pltpu.SemaphoreType.DMA((kinds, C)),
             pltpu.SemaphoreType.DMA((m - 1, C)),
@@ -531,28 +579,28 @@
         compiler_params=pltpu.CompilerParams(
             collective_id=0, has_side_effects=True, vmem_limit_bytes=VMEM_BYTES - size
         ),
-    )(up, down, pup, pdown, vec)
-    half_up, half_down, new_up, new_down = pl.pallas_call(
+    )(up, down, pup, pdown, slope_norm, slope_bias, pnorm, pbias)
+    half_up, half_down, half_norm, half_bias, new_up, new_down, next_norm, next_bias = pl.pallas_call(
         put_kernel,
         out_shape=(
             jax.ShapeDtypeStruct((Z, 2, CH, R, L), BF16),
             jax.ShapeDtypeStruct((L, n * rows), BF16),
+            jax.ShapeDtypeStruct((width,), BF16),
+            jax.ShapeDtypeStruct((width,), BF16),
             jax.ShapeDtypeStruct((CH, R, L), F32),
             jax.ShapeDtypeStruct((CH, R, L), F32),
+            jax.ShapeDtypeStruct((rows,), F32),
+            jax.ShapeDtypeStruct((rows,), F32),
         ),
-        in_specs=[vmem] * 3,
-        out_specs=(hbm,) * 4,
+        in_specs=[vmem] * 4,
+        out_specs=(hbm, hbm, vmem, vmem, hbm, hbm, vmem, vmem),
         scratch_shapes=[pltpu.SemaphoreType.DMA((4 * Z + 2,))],
         compiler_params=pltpu.CompilerParams(vmem_limit_bytes=1 << 20),
-    )(*(pltpu.with_memory_space_constraint(x, pltpu.VMEM) for x in (G, T, NX)))
+    )(*(pltpu.with_memory_space_constraint(x, pltpu.VMEM) for x in (G, T, NX, sums)))
     half_up = half_up.reshape(n * rows, L)
     next_up = new_up.reshape(rows, L)
     next_down = new_down.reshape(rows, L).T
-    sums = sums.reshape(4, width)
-    whole = sums[2:] - learn_rate * (sums[:2] * n ** (-0.5))
-    own = lax.dynamic_slice_in_dim(whole, place * rows, rows, axis=1)
-    halves = whole.astype(BF16)
-    return (half_up, half_down, halves[0], halves[1], next_up, next_down, own[0], own[1])
+    return (half_up, half_down, half_norm, half_bias, next_up, next_down, next_norm, next_bias)
 
 
 def solution(mesh):

time: 252 us -> 248 us (0.984)
  no operation moved by 1% of the time
where the time goes in v2:
time: 248 us
  Pallas kernels  247 us (100%)
    pallas_call x1, Pallas kernels, on_device(): pl.pallas_call(functools.partial(kernel, n, m, LA), out_shape=tuple((pltp...  241 us
    pallas_call x1, Pallas kernels, on_device(): pl.pallas_call(put_kernel, out_shape=(jax.ShapeDtypeStruct((Z, 2, CH, R,...  6.5 us

profile of v2, /device:TPU:0, one launch (start us, length us, event | category | flops | bytes accessed | tf_op | source)
XLA Modules:
  0.0 247.7 jit_solution(14727185463830131479)
XLA Ops:
  0.6 240.6 %shard_map.143 = (bf16[4,2,40,8,2560]{4,3,2,1,0:T(8,128)(2,1)S(1)}, bf16[2560,1280]{1,0:T(8,128)(2,1)S(1)}, f32[40,8,2560]{2,1,0:T(8,128)S(1)}, f32[4,1280]{1,0:T(4,128)S(1)}) custom-call(f32[4,2,20,8,2560]{4,3,2,1,0:T(8,128)} %bitcast.13, f32[2560,1280]{1,0:T(8,128)} %bitcast.14, f32[20,8,2560]{2,1,0:T(8,128)} %bitcast.15, f32[20,8,2560]{2,1,0:T(8,128)} %bitcast.16, ...), custom_call_target="tpu_custom_call" | custom-call | tf_op jit(solution)/shard_map/pallas_call | solution.py:549
  241.2 6.5 %shard_map.144 = (bf16[4,2,20,8,2560]{4,3,2,1,0:T(8,128)(2,1)}, bf16[2560,1280]{1,0:T(8,128)(2,1)}, bf16[1280]{0:T(1024)(128)(2,1)}, bf16[1280]{0:T(1024)(128)(2...) custom-call(bf16[4,2,40,8,2560]{4,3,2,1,0:T(8,128)(2,1)S(1)} %get-tuple-element.20.G, ...), custom_call_target="tpu_custom_call" | custom-call | tf_op jit(solution)/shard_map/pallas_call | solution.py:583

commit v3 on v2

v3 whole, which is shorter than its diff:
```python
import functools
import math

import jax
import jax.numpy as jnp
from jax import lax
from jax.experimental import pallas as pl
from jax.experimental.pallas import tpu as pltpu
from jax.sharding import PartitionSpec as P

learn_rate = 0.4
MESH = pl.DeviceIdType.MESH
R = 8
LANE = 128
SPLIT = 0.6
HEAD, TAIL = 1, 2
DEPTH = 4
SENDS = 2
VMEM_BYTES = 66_000_000
F32, BF16 = jnp.float32, jnp.bfloat16


def kernel(
    n,
    m,
    LA,
    up_ref,
    down_ref,
    pup_ref,
    pdown_ref,
    norm_ref,
    bias_ref,
    pnorm_ref,
    pbias_ref,
    G,
    T,
    NX,
    half_norm_ref,
    half_bias_ref,
    next_norm_ref,
    next_bias_ref,
    stage,
    turn,
    XA,
    XB,
    RYA,
    RYB,
    RZA,
    RZB,
    PR,
    SQ,
    V,
    VP,
    VY,
    VZ,
    up_sem,
    down_sem,
    par_sem,
    send,
    recv,
    sum_recv,
    gather_recv,
    gather_send,
    sq_send,
    sq_recv,
    v_send,
    v_recv,
):
    Z = n // 2
    C = NX.shape[0]
    CH = C // 2
    H0 = CH // 2
    L = NX.shape[2]
    me = lax.axis_index("batch")
    core = lax.axis_index("cols")
    z = me // 2
    y = me % 2
    other = z * 2 + 1 - y
    rate = n ** (-0.5)

    def slot(p):
        return jnp.where(p < H0, p, jnp.where(p < H0 + CH, p - H0 + CH, p - CH))

    def load_up(c):
        return pltpu.make_async_copy(up_ref.at[:, :, c], stage.at[c % 2], up_sem.at[c % 2])

    blocks = L // LANE
    share = -(-blocks // H0)
    back = -(-blocks // (CH - H0))

    def load_down(b):
        return pltpu.make_async_copy(
            down_ref.at[pl.ds(b * LANE, LANE)], turn.at[b % DEPTH], down_sem.at[b % DEPTH]
        )

    def turn_block(b):
        def pieces(store):
            for j in range(n * CH * R // LANE):
                tile = turn[b % DEPTH, :, j * LANE : (j + 1) * LANE].T
                for i in range(LANE // R):
                    piece = j * (LANE // R) + i
                    d, k = piece // CH, piece % CH
                    store(d // 2, d % 2, CH + k, tile[i * R : (i + 1) * R].astype(BF16))

        @pl.when(b * LANE < LA)
        def _():
            at = pl.ds(pl.multiple_of(b * LANE, LANE), LANE)

            def store(d, v, c, x):
                XA[c, v, d, :, at] = x

            pieces(store)

        @pl.when(b * LANE >= LA)
        def _():
            at = pl.ds(pl.multiple_of(b * LANE - LA, LANE), LANE)

            def store(d, v, c, x):
                XB[c, d, v, :, at] = x

            pieces(store)

    def load_params():
        return [
            pltpu.make_async_copy(pup_ref, PR.at[pl.ds(0, CH)], par_sem.at[0]),
            pltpu.make_async_copy(pdown_ref, PR.at[pl.ds(CH, CH)], par_sem.at[1]),
        ]

    def load_vectors():
        return [
            pltpu.make_async_copy(norm_ref, V.at[0], par_sem.at[2]),
            pltpu.make_async_copy(bias_ref, V.at[1], par_sem.at[3]),
            pltpu.make_async_copy(pnorm_ref, VP.at[0], par_sem.at[4]),
            pltpu.make_async_copy(pbias_ref, VP.at[1], par_sem.at[5]),
        ]

    load_up(0).start()
    for d in load_params() + load_vectors():
        d.start()

    for b in range(min(DEPTH - 1, blocks)):
        load_down(b).start()

    barrier = pltpu.get_barrier_semaphore()
    def greet(to):
        pl.semaphore_signal(barrier, inc=1, device_id={"batch": to}, device_id_type=MESH)

    greet(other)

    @pl.when(z > 0)
    def _():
        greet(me - 2)

    @pl.when(z < Z - 1)
    def _():
        greet(me + 2)

    for o in range(1, m):
        pl.semaphore_signal(
            barrier, inc=1, device_id={"cols": (core + o) % m}, device_id_type=MESH
        )
    pl.semaphore_wait(barrier, jnp.where((z == 0) | (z == Z - 1), m + 1, m + 2))

    waits = recv.shape[1]

    def remote(src, dst, kind, p, to):
        return pltpu.make_async_remote_copy(
            src_ref=src,
            dst_ref=dst,
            send_sem=send.at[kind, p % SENDS],
            recv_sem=recv.at[kind, p % waits],
            device_id={"batch": to},
            device_id_type=MESH,
        )

    def free(copy, p):
        @pl.when(p >= SENDS)
        def _():
            copy(p - SENDS).wait_send()

    def go(copy, p):
        free(copy, p)
        copy(p).start()

    def vec_y():
        return pltpu.make_async_remote_copy(
            src_ref=VZ.at[z],
            dst_ref=VY,
            send_sem=v_send.at[0],
            recv_sem=v_recv.at[0],
            device_id={"batch": other},
            device_id_type=MESH,
        )

    def vec_z(side, lo, count, to):
        ref = VZ.at[pl.ds(lo, count)]
        return pltpu.make_async_remote_copy(
            src_ref=ref,
            dst_ref=ref,
            send_sem=v_send.at[side],
            recv_sem=v_recv.at[side],
            device_id={"batch": to},
            device_id_type=MESH,
        )

    def vec_right(k):
        return vec_z(1, 0, k + 1, jnp.minimum(me + 2, n - 1))

    def vec_left(k):
        return vec_z(2, k, Z - k, jnp.maximum(me - 2, 0))

    def vec_step(t):
        for k in range(Z):

            @pl.when((z == k) & (t == k))
            def _():
                if k > 0:
                    vec_right(k - 1).wait_recv()
                if k < Z - 1:
                    vec_right(k).start()

            @pl.when((z == k) & (t == Z - 1 - k))
            def _():
                if k < Z - 1:
                    vec_left(k + 1).wait_recv()
                if k > 0:
                    vec_left(k).start()

            @pl.when((z == k) & (t == Z))
            def _():
                if k < Z - 1:
                    vec_right(k).wait_send()
                if k > 0:
                    vec_left(k).wait_send()

        @pl.when(t == Z)
        def _():
            total = VZ[0]
            for k in range(1, Z):
                total = total + VZ[k]
            width = VZ.shape[2]
            rows = width // n
            whole = total[2:4] - learn_rate * (total[0:2] * rate)
            halves = whole.astype(BF16)
            half_norm_ref[...] = halves[0:1].reshape(width)
            half_bias_ref[...] = halves[1:2].reshape(width)
            own = pltpu.roll(whole, (n - me) % n * rows, 1)[:, :rows]
            next_norm_ref[...] = own[0:1].reshape(rows)
            next_bias_ref[...] = own[1:2].reshape(rows)

    def sq_copy(p, o):
        return pltpu.make_async_remote_copy(
            src_ref=SQ.at[slot(p), 0],
            dst_ref=SQ.at[slot(p), o],
            send_sem=sq_send.at[o - 1, p % SENDS],
            recv_sem=sq_recv.at[o - 1, p % waits],
            device_id={"cols": (core + o) % m},
            device_id_type=MESH,
        )

    YA, YB, RA, LFA, RB, LFB, GYA, GYB, GRA, GLA, GRB, GLB = range(12)

    def ya(p):
        c = slot(p)
        return remote(XA.at[c, 1 - y], RYA.at[c], YA, p, other)

    def yb(p):
        c = slot(p)
        return remote(XB.at[c, z, 1 - y], RYB.at[c], YB, p, other)

    def gya(p):
        ref = G.at[:, y, slot(p), :, pl.ds(0, LA)]
        return remote(ref, ref, GYA, p, other)

    def gya_in(p):
        ref = G.at[:, 1 - y, slot(p), :, pl.ds(0, LA)]
        return remote(ref, ref, GYA, p, other)

    def gyb(p):
        ref = G.at[z, y, slot(p), :, pl.ds(LA, L - LA)]
        return remote(ref, ref, GYB, p, other)

    def gyb_in(p):
        ref = G.at[z, 1 - y, slot(p), :, pl.ds(LA, L - LA)]
        return remote(ref, ref, GYB, p, other)

    def head(p):
        return p < HEAD

    def tail(p):
        return p >= C - TAIL

    def right_of():
        return jnp.minimum(me + 2, n - 1)

    def left_of():
        return jnp.maximum(me - 2, 0)

    def piece(src, dst, send_sem, recv_sem, to):
        return pltpu.make_async_remote_copy(
            src_ref=src,
            dst_ref=dst,
            send_sem=send_sem,
            recv_sem=recv_sem,
            device_id={"batch": to},
            device_id_type=MESH,
        )

    def sum_piece(first, right, p, d):
        c = slot(p)
        rz = RZA if first else RZB
        kind = (RA if first else RB) if right else (LFA if first else LFB)
        return piece(
            XA.at[c, y, d] if first else XB.at[c, d],
            rz.at[c, d + 1 if right else d],
            send.at[kind, p % SENDS],
            sum_recv.at[2 * first + right, p, d],
            right_of() if right else left_of(),
        )

    def gather_piece(first, right, p, d):
        kind = (GRA if first else GRB) if right else (GLA if first else GLB)
        if first:
            ref = G.at[d, y, slot(p), :, pl.ds(0, LA)]
        else:
            ref = G.at[d, :, slot(p), :, pl.ds(LA, L - LA)]
        return piece(
            ref,
            ref,
            send.at[kind, p % SENDS],
            gather_recv.at[2 * first + right, p - (C - TAIL), d],
            right_of() if right else left_of(),
        )

    def gya_piece(p, d, v):
        ref = G.at[d, v, slot(p), :, pl.ds(0, LA)]
        e = p - (C - TAIL)
        return piece(ref, ref, gather_send.at[e, d], gather_recv.at[4, e, d], other)

    def x_ref(first, c):
        return XA.at[c, y] if first else XB.at[c]

    def sum_right(first, p, k):
        c = slot(p)
        rz = RZA if first else RZB
        return remote(
            x_ref(first, c).at[pl.ds(k + 1, Z - 1 - k)],
            rz.at[c, pl.ds(k + 2, Z - 1 - k)],
            RA if first else RB,
            p,
            right_of(),
        )

    def sum_left(first, p, k):
        c = slot(p)
        rz = RZA if first else RZB
        return remote(
            x_ref(first, c).at[pl.ds(0, k)],
            rz.at[c, pl.ds(0, k)],
            LFA if first else LFB,
            p,
            left_of(),
        )

    def add(first, p, lo, count, at):
        c = slot(p)
        rz = RZA if first else RZB
        for d in range(count):
            if first:
                XA[c, y, lo + d] = (
                    XA[c, y, lo + d].astype(F32) + rz[c, at + d].astype(F32)
                ).astype(BF16)
            else:
                XB[c, lo + d] = (
                    XB[c, lo + d].astype(F32) + rz[c, at + d].astype(F32)
                ).astype(BF16)

    def at_hop(t, k, bulk, pieces, special):
        for right in (True, False):
            p = t - k if right else t - (Z - 1 - k)
            here = (z == k) & (p >= 0) & (p < C)

            @pl.when(here & jnp.logical_not(special(p)))
            def _():
                bulk(right, p)

            @pl.when(here & special(p))
            def _():
                pieces(right, p)

    def reduce_step(first, t):
        for k in range(Z):

            def to_right(p):
                return sum_right(first, p, k)

            def to_left(p):
                return sum_left(first, p, k)

            def bulk(right, p):
                if right:
                    if k > 0:
                        sum_right(first, p, k - 1).wait_recv()
                        add(first, p, k, Z - k, k + 1)
                    if k < Z - 1:
                        go(to_right, p)
                else:
                    if k < Z - 1:
                        sum_left(first, p, k + 1).wait_recv()
                        add(first, p, 0, k + 1, 0)
                    if k > 0:
                        go(to_left, p)

            def pieces(right, p):
                if k < Z - 1 if right else k > 0:
                    free(to_right if right else to_left, p)
                for d in range(Z - 1, k - 1, -1) if right else range(k + 1):
                    if k > 0 if right else k < Z - 1:
                        sum_piece(first, right, p, d).wait_recv()
                        add(first, p, d, 1, d + 1 if right else d)
                    if d != k:
                        sum_piece(first, right, p, d).start()

            at_hop(t, k, bulk, pieces, head)

    def g_ref(first, c, lo, count):
        at = pl.ds(lo, count)
        if first:
            return G.at[at, y, c, :, pl.ds(0, LA)]
        return G.at[at, :, c, :, pl.ds(LA, L - LA)]

    def gather_right(first, p, k):
        ref = g_ref(first, slot(p), 0, k + 1)
        return remote(ref, ref, GRA if first else GRB, p, right_of())

    def gather_left(first, p, k):
        ref = g_ref(first, slot(p), k, Z - k)
        return remote(ref, ref, GLA if first else GLB, p, left_of())

    def gather_step(first, t):
        for k in range(Z):

            def to_right(p):
                return gather_right(first, p, k)

            def to_left(p):
                return gather_left(first, p, k)

            def bulk(right, p):
                if right:
                    if k > 0:
                        gather_right(first, p, k - 1).wait_recv()
                    if k < Z - 1:
                        go(to_right, p)
                else:
                    if k < Z - 1:
                        gather_left(first, p, k + 1).wait_recv()
                    if k > 0:
                        go(to_left, p)

            def pieces(right, p):
                on = k < Z - 1 if right else k > 0
                if on:
                    free(to_right if right else to_left, p)
                for d in range(k, -1, -1) if right else range(k, Z):
                    if d != k:
                        gather_piece(first, right, p, d).wait_recv()
                    if on:
                        gather_piece(first, right, p, d).start()
                    if first and d != k:
                        gya_piece(p, d, y).start()

            at_hop(t, k, bulk, pieces, tail)

    def last_sends(p):
        for copy in (ya, yb, gyb):
            copy(p).wait_send()
        for o in range(1, m):
            sq_copy(p, o).wait_send()
        for k in range(Z):

            @pl.when(z == k)
            def _():
                for first in (True, False):
                    if k < Z - 1:
                        sum_right(first, p, k).wait_send()
                        gather_right(first, p, k).wait_send()
                    if k > 0:
                        sum_left(first, p, k).wait_send()
                        gather_left(first, p, k).wait_send()

    def back_block(b):
        at = pl.ds(pl.multiple_of(b * LANE, LANE), LANE)
        for j in range(n * CH * R // LANE):
            rows = []
            for i in range(LANE // R):
                piece = j * (LANE // R) + i
                d, k = piece // CH, piece % CH
                rows.append(G[d // 2, d % 2, CH + k, :, at].astype(F32))
            tile = jnp.concatenate(rows, axis=0)
            T[at, j * LANE : (j + 1) * LANE] = tile.T.astype(BF16)

    def lanes(x):
        s = x[:, :LANE] * x[:, :LANE]
        for i in range(1, L // LANE):
            part = x[:, i * LANE : (i + 1) * LANE]
            s = s + part * part
        return s

    def when_chunk(c):
        return pl.when((c >= 0) & (c < C))

    @pl.loop(0, C + 2 * Z)
    def _(t):
        def load_at(p, act):
            @pl.when((p < H0) | ((p >= H0 + CH) & (p < C)))
            def _():
                act(slot(p))

        load_at(t + 1, lambda c: load_up(c).start())

        def cast(c):
            load_up(c).wait()
            for d in range(Z):
                for v in range(2):
                    XA[c, v, d] = stage[c % 2, d, v, :, :LA].astype(BF16)
                    XB[c, d, v] = stage[c % 2, d, v, :, LA:].astype(BF16)

        load_at(t, cast)

        @pl.when(t < C)
        def _():
            go(ya, t)

        reduce_step(False, t)
        s = t - 1

        @pl.when(t == 0)
        def _():
            for d in load_vectors():
                d.wait()
            width = VY.shape[1]
            place = jnp.zeros((1, width - VP.shape[2]), F32)
            for i in range(2):
                VZ[z, i : i + 1] = V[i]
                own = jnp.concatenate([VP[i], place], axis=1)
                VZ[z, 2 + i : 3 + i] = pltpu.roll(own, me * VP.shape[2], 1)
            vec_y().start()

        @pl.when(t == 1)
        def _():
            vec_y().wait()
            VZ[z] = VZ[z] + VY[...]

        @when_chunk(s)
        def _():
            c = slot(s)
            ya(s).wait_recv()
            for d in range(Z):
                XA[c, y, d] = (XA[c, y, d].astype(F32) + RYA[c, d].astype(F32)).astype(BF16)

        reduce_step(True, s)
        b = t - (Z - 1)

        @when_chunk(b)
        def _():
            go(yb, b)

        u = t - Z

        @pl.when(u == 0)
        def _():
            for d in load_params():
                d.wait()

        @when_chunk(u)
        def _():
            f = slot(u)
            yb(u).wait_recv()
            NX[f, :, :LA] = XA[f, y, z].astype(F32) * rate
            NX[f, :, LA:] = (XB[f, z, y].astype(F32) + RYB[f].astype(F32)) * rate
            SQ[f, 0, 0] = lanes(NX[f])
            SQ[f, 0, 1] = lanes(PR[f])
            for o in range(1, m):
                go(lambda p, o=o: sq_copy(p, o), u)

        @when_chunk(u - 1)
        def _():
            gyb_in(u - 1).wait_recv()

        gather_step(False, u - 1)
        e = u - Z

        @when_chunk(u)
        def _():
            f = slot(u)
            for o in range(1, m):
                sq_copy(u, o).wait_recv()
            g = SQ[f, 0, 0]
            p = SQ[f, 0, 1]
            for o in range(1, m):
                g = g + SQ[f, o, 0]
                p = p + SQ[f, o, 1]
            g = jnp.sum(g, axis=1, keepdims=True)
            p = jnp.sum(p, axis=1, keepdims=True)
            scale = learn_rate * (jnp.sqrt(p) * lax.rsqrt(g + 1e-06))
            new = PR[f] - NX[f] * scale
            NX[f] = new
            G[z, y, f] = new.astype(BF16)
            go(gyb, u)

            @pl.when(tail(u))
            def _():
                gya_piece(u, z, y).start()

        gather_step(True, u)

        w = u - (Z - 1)

        @pl.when((w >= 0) & jnp.logical_not(tail(w)))
        def _():
            go(gya, w)

        vec_step(t - 1)

        @pl.when((e >= 0) & jnp.logical_not(tail(e)))
        def _():
            gya_in(e).wait_recv()

        @pl.when((e < C) & tail(e))
        def _():
            for d in range(Z):
                gya_piece(e, d, 1 - y).wait_recv()
                gya_piece(e, d, y).wait_send()

        for i in range(share):
            b = t * share + i

            @pl.when(b + DEPTH - 1 < blocks)
            def _():
                load_down(b + DEPTH - 1).start()

            @pl.when(b < blocks)
            def _():
                load_down(b).wait()
                turn_block(b)

        for i in range(back):
            w = (t - (H0 + CH + 2 * Z)) * back + i

            @pl.when((w >= 0) & (w < blocks))
            def _():
                back_block(w)

    for i in range(SENDS):
        last_sends(C - SENDS + i)
        gya(C - TAIL - SENDS + i).wait_send()


def put_kernel(
    G,
    T,
    NX,
    half_norm,
    half_bias,
    next_norm,
    next_bias,
    half_up_ref,
    half_down_ref,
    half_norm_ref,
    half_bias_ref,
    next_up_ref,
    next_down_ref,
    next_norm_ref,
    next_bias_ref,
    sem,
):
    Z = G.shape[0]
    CH = G.shape[2] // 2
    part = T.shape[0] // (2 * Z)
    copies = []

    def put(src, dst):
        d = pltpu.make_async_copy(src, dst, sem.at[len(copies)])
        d.start()
        copies.append(d)

    for k in range(Z):
        for v in range(2):
            put(G.at[k, v, pl.ds(0, CH)], half_up_ref.at[k, v])
            at = pl.ds((2 * k + v) * part, part)
            put(T.at[at], half_down_ref.at[at])
    put(NX.at[pl.ds(0, CH)], next_up_ref)
    put(NX.at[pl.ds(CH, CH)], next_down_ref)
    put(half_norm, half_norm_ref)
    put(half_bias, half_bias_ref)
    put(next_norm, next_norm_ref)
    put(next_bias, next_bias_ref)
    for d in copies:
        d.wait()


def on_device(
    slope_up, slope_down, slope_norm, slope_bias, param_up, param_down, param_norm, param_bias
):
    n = lax.axis_size("batch")
    m = lax.axis_size("cols")
    Z = n // 2
    rows, L = param_up.shape
    CH = rows // R
    C = 2 * CH
    LA = max(1, round(SPLIT * L / LANE)) * LANE
    LB = L - LA
    width = slope_norm.shape[1]
    up = slope_up[0].reshape(Z, 2, CH, R, L)
    down = slope_down[0]
    pup = param_up.reshape(CH, R, L)
    pdown = param_down.T.reshape(CH, R, L)
    pnorm = param_norm.reshape(1, rows)
    pbias = param_bias.reshape(1, rows)
    hbm = pl.BlockSpec(memory_space=pl.ANY)
    vmem = pl.BlockSpec(memory_space=pltpu.VMEM)
    kept = [((Z, 2, C, R, L), BF16), ((L, n * rows), BF16), ((C, R, L), F32)]
    kept += [((width,), BF16)] * 2 + [((rows,), F32)] * 2
    size = sum(jnp.dtype(dtype).itemsize * math.prod(shape) for shape, dtype in kept)
    held = pl.pallas_call(
        functools.partial(kernel, n, m, LA),
        out_shape=tuple(pltpu.VMEM(shape, dtype) for shape, dtype in kept),
        in_specs=[hbm] * 8,
        out_specs=(vmem,) * 7,
        scratch_shapes=[
            pltpu.VMEM((2, Z, 2, R, L), F32),
            pltpu.VMEM((DEPTH, LANE, n * rows), F32),
            pltpu.VMEM((C, 2, Z, R, LA), BF16),
            pltpu.VMEM((C, Z, 2, R, LB), BF16),
            pltpu.VMEM((C, Z, R, LA), BF16),
            pltpu.VMEM((C, R, LB), BF16),
            pltpu.VMEM((C, Z + 1, R, LA), BF16),
            pltpu.VMEM((C, Z + 1, 2, R, LB), BF16),
            pltpu.VMEM((C, R, L), F32),
            pltpu.VMEM((C, m, 2, R, LANE), F32),
            pltpu.VMEM((2, 1, width), F32),
            pltpu.VMEM((2, 1, rows), F32),
            pltpu.VMEM((4, width), F32),
            pltpu.VMEM((Z, 4, width), F32),
            pltpu.SemaphoreType.DMA((2,)),
            pltpu.SemaphoreType.DMA((DEPTH,)),
            pltpu.SemaphoreType.DMA((6,)),
            pltpu.SemaphoreType.DMA((12, SENDS)),
            pltpu.SemaphoreType.DMA((12, Z + 2)),
            pltpu.SemaphoreType.DMA((4, HEAD, Z)),
            pltpu.SemaphoreType.DMA((5, TAIL, Z)),
            pltpu.SemaphoreType.DMA((TAIL, Z)),
            pltpu.SemaphoreType.DMA((m - 1, SENDS)),
            pltpu.SemaphoreType.DMA((m - 1, Z + 2)),
            pltpu.SemaphoreType.DMA((3,)),
            pltpu.SemaphoreType.DMA((3,)),
        ],
        compiler_params=pltpu.CompilerParams(
            collective_id=0, has_side_effects=True, vmem_limit_bytes=VMEM_BYTES - size
        ),
    )(up, down, pup, pdown, slope_norm, slope_bias, pnorm, pbias)
    half_up, half_down, half_norm, half_bias, new_up, new_down, next_norm, next_bias = pl.pallas_call(
        put_kernel,
        out_shape=(
            jax.ShapeDtypeStruct((Z, 2, CH, R, L), BF16),
            jax.ShapeDtypeStruct((L, n * rows), BF16),
            jax.ShapeDtypeStruct((width,), BF16),
            jax.ShapeDtypeStruct((width,), BF16),
            jax.ShapeDtypeStruct((CH, R, L), F32),
            jax.ShapeDtypeStruct((CH, R, L), F32),
            jax.ShapeDtypeStruct((rows,), F32),
            jax.ShapeDtypeStruct((rows,), F32),
        ),
        in_specs=[vmem] * 7,
        out_specs=(hbm,) * 8,
        scratch_shapes=[pltpu.SemaphoreType.DMA((4 * Z + 6,))],
        compiler_params=pltpu.CompilerParams(vmem_limit_bytes=1 << 20),
    )(*(pltpu.with_memory_space_constraint(x, pltpu.VMEM) for x in held))
    half_up = half_up.reshape(n * rows, L)
    next_up = new_up.reshape(rows, L)
    next_down = new_down.reshape(rows, L).T
    return (half_up, half_down, half_norm, half_bias, next_up, next_down, next_norm, next_bias)


def solution(mesh):
    return jax.shard_map(
        on_device,
        mesh=mesh,
        in_specs=(
            P(("ens", "batch"), None, "cols"),
            P(("ens", "batch"), "cols", None),
            P(("ens", "batch"), None),
            P(("ens", "batch"), None),
            P(("ens", "batch"), "cols"),
            P(("ens", "cols"), "batch"),
            P(("ens", "batch")),
            P(("ens", "batch")),
        ),
        out_specs=(
            P("ens", "cols"),
            P(("ens", "cols"), None),
            P("ens"),
            P("ens"),
            P(("ens", "batch"), "cols"),
            P(("ens", "cols"), "batch"),
            P(("ens", "batch")),
            P(("ens", "batch")),
        ),
        check_vma=False,
    )
```

time: 248 us -> 235 us (0.948)
  Pallas kernels: 247 us -> 234 us
    pallas_call x1, Pallas kernels: 241 us -> 228 us  [on_device(): pl.pallas_call(functools.partial(kernel, n, m, LA), out_shape=tuple((pltp...]
where the time goes in v3:
time: 235 us
  Pallas kernels  234 us (100%)
    pallas_call x1, Pallas kernels, on_device(): pl.pallas_call(functools.partial(kernel, n, m, LA), out_shape=tuple((pltp...  228 us
    pallas_call x1, Pallas kernels, on_device(): pl.pallas_call(put_kernel, out_shape=(jax.ShapeDtypeStruct((Z, 2, CH, R,...  5.95 us

profile of v3, /device:TPU:0, one launch (start us, length us, event | category | flops | bytes accessed | tf_op | source)
XLA Modules:
  0.0 235.0 jit_solution(13685764058203730408)
XLA Ops:
  0.6 228.4 %shard_map.143 = (bf16[4,2,40,8,2560]{4,3,2,1,0:T(8,128)(2,1)S(1)}, bf16[2560,1280]{1,0:T(8,128)(2,1)S(1)}, f32[40,8,2560]{2,1,0:T(8,128)S(1)}, bf16[1280]{0:T(1...) custom-call(f32[4,2,20,8,2560]{4,3,2,1,0:T(8,128)} %bitcast.13, ...), custom_call_target="tpu_custom_call" | custom-call | tf_op jit(solution)/shard_map/pallas_call | solution.py:726
  229.1 5.9 %shard_map.144 = (bf16[4,2,20,8,2560]{4,3,2,1,0:T(8,128)(2,1)}, bf16[2560,1280]{1,0:T(8,128)(2,1)}, bf16[1280]{0:T(1024)(128)(2,1)}, bf16[1280]{0:T(1024)(128)(2...) custom-call(bf16[4,2,40,8,2560]{4,3,2,1,0:T(8,128)(2,1)S(1)} %get-tuple-element.23.G, ...), custom_call_target="tpu_custom_call" | custom-call | tf_op jit(solution)/shard_map/pallas_call | solution.py:763

commit v4 on v3

--- a/solution.py
+++ b/solution.py
@@ -13,9 +13,10 @@
 R = 8
 LANE = 128
 SPLIT = 0.6
-HEAD, TAIL = 1, 2
+HEAD, TAIL = 1, 1
 DEPTH = 4
 SENDS = 2
+LAST, LAST_SPLIT = 6, 0.75
 VMEM_BYTES = 66_000_000
 F32, BF16 = jnp.float32, jnp.bfloat16
 
@@ -24,6 +25,7 @@
     n,
     m,
     LA,
+    LW,
     up_ref,
     down_ref,
     pup_ref,
@@ -58,6 +60,7 @@
     par_sem,
     send,
     recv,
+    first_recv,
     sum_recv,
     gather_recv,
     gather_send,
@@ -182,6 +185,27 @@
         free(copy, p)
         copy(p).start()
 
+    def wide(p):
+        return p >= C - LAST
+
+    def split(p, act):
+        @pl.when(jnp.logical_not(wide(p)))
+        def _():
+            act(LA)
+
+        @pl.when(wide(p))
+        def _():
+            act(LW)
+
+    def free_split(copy, p):
+        @pl.when(p >= SENDS)
+        def _():
+            split(p - SENDS, lambda la: copy(p - SENDS, la).wait_send())
+
+    def go_split(copy, p):
+        free_split(copy, p)
+        split(p, lambda la: copy(p, la).start())
+
     def vec_y():
         return pltpu.make_async_remote_copy(
             src_ref=VZ.at[z],
@@ -268,20 +292,20 @@
         c = slot(p)
         return remote(XB.at[c, z, 1 - y], RYB.at[c], YB, p, other)
 
-    def gya(p):
-        ref = G.at[:, y, slot(p), :, pl.ds(0, LA)]
+    def gya(p, la):
+        ref = G.at[:, y, slot(p), :, pl.ds(0, la)]
         return remote(ref, ref, GYA, p, other)
 
-    def gya_in(p):
-        ref = G.at[:, 1 - y, slot(p), :, pl.ds(0, LA)]
+    def gya_in(p, la):
+        ref = G.at[:, 1 - y, slot(p), :, pl.ds(0, la)]
         return remote(ref, ref, GYA, p, other)
 
-    def gyb(p):
-        ref = G.at[z, y, slot(p), :, pl.ds(LA, L - LA)]
+    def gyb(p, la):
+        ref = G.at[z, y, slot(p), :, pl.ds(la, L - la)]
         return remote(ref, ref, GYB, p, other)
 
-    def gyb_in(p):
-        ref = G.at[z, 1 - y, slot(p), :, pl.ds(LA, L - LA)]
+    def gyb_in(p, la):
+        ref = G.at[z, 1 - y, slot(p), :, pl.ds(la, L - la)]
         return remote(ref, ref, GYB, p, other)
 
     def head(p):
@@ -305,6 +329,23 @@
             device_id={"batch": to},
             device_id_type=MESH,
         )
+
+    def ya_piece(p, d):
+        c = slot(p)
+        return piece(
+            XA.at[c, 1 - y, d],
+            RYA.at[c, d],
+            send.at[YA, p % SENDS],
+            first_recv.at[p, d],
+            other,
+        )
+
+    def take(p, d):
+        c = slot(p)
+        ya_piece(p, d).wait_recv()
+        XA[c, y, d] = (XA[c, y, d].astype(F32) + RYA[c, d].astype(F32)).astype(BF16)
+
+    inward = [d for i in range(Z // 2) for d in (Z - 1 - i, i)]
 
     def sum_piece(first, right, p, d):
         c = slot(p)
@@ -321,9 +362,9 @@
     def gather_piece(first, right, p, d):
         kind = (GRA if first else GRB) if right else (GLA if first else GLB)
         if first:
-            ref = G.at[d, y, slot(p), :, pl.ds(0, LA)]
+            ref = G.at[d, y, slot(p), :, pl.ds(0, LW)]
         else:
-            ref = G.at[d, :, slot(p), :, pl.ds(LA, L - LA)]
+            ref = G.at[d, :, slot(p), :, pl.ds(LW, L - LW)]
         return piece(
             ref,
             ref,
@@ -333,7 +374,7 @@
         )
 
     def gya_piece(p, d, v):
-        ref = G.at[d, v, slot(p), :, pl.ds(0, LA)]
+        ref = G.at[d, v, slot(p), :, pl.ds(0, LW)]
         e = p - (C - TAIL)
         return piece(ref, ref, gather_send.at[e, d], gather_recv.at[4, e, d], other)
 
@@ -415,6 +456,8 @@
                 if k < Z - 1 if right else k > 0:
                     free(to_right if right else to_left, p)
                 for d in range(Z - 1, k - 1, -1) if right else range(k + 1):
+                    if first and k == (0 if right else Z - 1):
+                        take(p, d)
                     if k > 0 if right else k < Z - 1:
                         sum_piece(first, right, p, d).wait_recv()
                         add(first, p, d, 1, d + 1 if right else d)
@@ -423,45 +466,45 @@
 
             at_hop(t, k, bulk, pieces, head)
 
-    def g_ref(first, c, lo, count):
+    def g_ref(first, c, lo, count, la):
         at = pl.ds(lo, count)
         if first:
-            return G.at[at, y, c, :, pl.ds(0, LA)]
-        return G.at[at, :, c, :, pl.ds(LA, L - LA)]
-
-    def gather_right(first, p, k):
-        ref = g_ref(first, slot(p), 0, k + 1)
+            return G.at[at, y, c, :, pl.ds(0, la)]
+        return G.at[at, :, c, :, pl.ds(la, L - la)]
+
+    def gather_right(first, p, k, la):
+        ref = g_ref(first, slot(p), 0, k + 1, la)
         return remote(ref, ref, GRA if first else GRB, p, right_of())
 
-    def gather_left(first, p, k):
-        ref = g_ref(first, slot(p), k, Z - k)
+    def gather_left(first, p, k, la):
+        ref = g_ref(first, slot(p), k, Z - k, la)
         return remote(ref, ref, GLA if first else GLB, p, left_of())
 
     def gather_step(first, t):
         for k in range(Z):
 
-            def to_right(p):
-                return gather_right(first, p, k)
-
-            def to_left(p):
-                return gather_left(first, p, k)
+            def to_right(p, la):
+                return gather_right(first, p, k, la)
+
+            def to_left(p, la):
+                return gather_left(first, p, k, la)
 
             def bulk(right, p):
                 if right:
                     if k > 0:
-                        gather_right(first, p, k - 1).wait_recv()
+                        split(p, lambda la: gather_right(first, p, k - 1, la).wait_recv())
                     if k < Z - 1:
-                        go(to_right, p)
+                        go_split(to_right, p)
                 else:
                     if k < Z - 1:
-                        gather_left(first, p, k + 1).wait_recv()
+                        split(p, lambda la: gather_left(first, p, k + 1, la).wait_recv())
                     if k > 0:
-                        go(to_left, p)
+                        go_split(to_left, p)
 
             def pieces(right, p):
                 on = k < Z - 1 if right else k > 0
                 if on:
-                    free(to_right if right else to_left, p)
+                    free_split(to_right if right else to_left, p)
                 for d in range(k, -1, -1) if right else range(k, Z):
                     if d != k:
                         gather_piece(first, right, p, d).wait_recv()
@@ -473,8 +516,8 @@
             at_hop(t, k, bulk, pieces, tail)
 
     def last_sends(p):
-        for copy in (ya, yb, gyb):
-            copy(p).wait_send()
+        for copy in (ya(p), yb(p), gyb(p, LW)):
+            copy.wait_send()
         for o in range(1, m):
             sq_copy(p, o).wait_send()
         for k in range(Z):
@@ -484,10 +527,10 @@
                 for first in (True, False):
                     if k < Z - 1:
                         sum_right(first, p, k).wait_send()
-                        gather_right(first, p, k).wait_send()
+                        gather_right(first, p, k, LW).wait_send()
                     if k > 0:
                         sum_left(first, p, k).wait_send()
-                        gather_left(first, p, k).wait_send()
+                        gather_left(first, p, k, LW).wait_send()
 
     def back_block(b):
         at = pl.ds(pl.multiple_of(b * LANE, LANE), LANE)
@@ -510,6 +553,14 @@
     def when_chunk(c):
         return pl.when((c >= 0) & (c < C))
 
+    def next_block(b):
+        @pl.when(b + DEPTH - 1 < blocks)
+        def _():
+            load_down(b + DEPTH - 1).start()
+
+        load_down(b).wait()
+        turn_block(b)
+
     @pl.loop(0, C + 2 * Z)
     def _(t):
         def load_at(p, act):
@@ -528,31 +579,29 @@
 
         load_at(t, cast)
 
-        @pl.when(t < C)
+        @pl.when((t < C) & jnp.logical_not(head(t)))
         def _():
             go(ya, t)
+
+        @pl.when(head(t))
+        def _():
+            free(ya, t)
+            for half in range(2):
+
+                @pl.when(z // (Z // 2) == half)
+                def _():
+                    for d in inward:
+                        ya_piece(t, Z - 1 - d if half else d).start()
 
         reduce_step(False, t)
         s = t - 1
 
-        @pl.when(t == 0)
-        def _():
-            for d in load_vectors():
-                d.wait()
-            width = VY.shape[1]
-            place = jnp.zeros((1, width - VP.shape[2]), F32)
-            for i in range(2):
-                VZ[z, i : i + 1] = V[i]
-                own = jnp.concatenate([VP[i], place], axis=1)
-                VZ[z, 2 + i : 3 + i] = pltpu.roll(own, me * VP.shape[2], 1)
-            vec_y().start()
-
-        @pl.when(t == 1)
-        def _():
-            vec_y().wait()
-            VZ[z] = VZ[z] + VY[...]
-
-        @when_chunk(s)
+        @pl.when((s >= 0) & head(s) & (z > 0) & (z < Z - 1))
+        def _():
+            for d in range(Z):
+                take(s, d)
+
+        @pl.when((s < C) & jnp.logical_not(head(s)))
         def _():
             c = slot(s)
             ya(s).wait_recv()
@@ -586,7 +635,7 @@
 
         @when_chunk(u - 1)
         def _():
-            gyb_in(u - 1).wait_recv()
+            split(u - 1, lambda la: gyb_in(u - 1, la).wait_recv())
 
         gather_step(False, u - 1)
         e = u - Z
@@ -607,7 +656,7 @@
             new = PR[f] - NX[f] * scale
             NX[f] = new
             G[z, y, f] = new.astype(BF16)
-            go(gyb, u)
+            go_split(gyb, u)
 
             @pl.when(tail(u))
             def _():
@@ -619,13 +668,30 @@
 
         @pl.when((w >= 0) & jnp.logical_not(tail(w)))
         def _():
-            go(gya, w)
-
-        vec_step(t - 1)
+            go_split(gya, w)
+
+        @pl.when(t == 0)
+        def _():
+            for d in load_vectors():
+                d.wait()
+            width = VY.shape[1]
+            place = jnp.zeros((1, width - VP.shape[2]), F32)
+            for i in range(2):
+                VZ[z, i : i + 1] = V[i]
+                own = jnp.concatenate([VP[i], place], axis=1)
+                VZ[z, 2 + i : 3 + i] = pltpu.roll(own, me * VP.shape[2], 1)
+            vec_y().start()
+
+        @pl.when(t == 2)
+        def _():
+            vec_y().wait()
+            VZ[z] = VZ[z] + VY[...]
+
+        vec_step(t - 3)
 
         @pl.when((e >= 0) & jnp.logical_not(tail(e)))
         def _():
-            gya_in(e).wait_recv()
+            split(e, lambda la: gya_in(e, la).wait_recv())
 
         @pl.when((e < C) & tail(e))
         def _():
@@ -636,14 +702,9 @@
         for i in range(share):
             b = t * share + i
 
-            @pl.when(b + DEPTH - 1 < blocks)
-            def _():
-                load_down(b + DEPTH - 1).start()
-
             @pl.when(b < blocks)
             def _():
-                load_down(b).wait()
-                turn_block(b)
+                next_block(b)
 
         for i in range(back):
             w = (t - (H0 + CH + 2 * Z)) * back + i
@@ -654,7 +715,7 @@
 
     for i in range(SENDS):
         last_sends(C - SENDS + i)
-        gya(C - TAIL - SENDS + i).wait_send()
+        gya(C - TAIL - SENDS + i, LW).wait_send()
 
 
 def put_kernel(
@@ -711,6 +772,7 @@
     C = 2 * CH
     LA = max(1, round(SPLIT * L / LANE)) * LANE
     LB = L - LA
+    LW = min(L // LANE - 1, round(LAST_SPLIT * L / LANE)) * LANE
     width = slope_norm.shape[1]
     up = slope_up[0].reshape(Z, 2, CH, R, L)
     down = slope_down[0]
@@ -724,7 +786,7 @@
     kept += [((width,), BF16)] * 2 + [((rows,), F32)] * 2
     size = sum(jnp.dtype(dtype).itemsize * math.prod(shape) for shape, dtype in kept)
     held = pl.pallas_call(
-        functools.partial(kernel, n, m, LA),
+        functools.partial(kernel, n, m, LA, LW),
         out_shape=tuple(pltpu.VMEM(shape, dtype) for shape, dtype in kept),
         in_specs=[hbm] * 8,
         out_specs=(vmem,) * 7,
@@ -748,6 +810,7 @@
             pltpu.SemaphoreType.DMA((6,)),
             pltpu.SemaphoreType.DMA((12, SENDS)),
             pltpu.SemaphoreType.DMA((12, Z + 2)),
+            pltpu.SemaphoreType.DMA((HEAD, Z)),
             pltpu.SemaphoreType.DMA((4, HEAD, Z)),
             pltpu.SemaphoreType.DMA((5, TAIL, Z)),
             pltpu.SemaphoreType.DMA((TAIL, Z)),

time: 235 us -> 233 us (level)
  no operation moved by 1% of the time
where the time goes in v4:
time: 233 us
  Pallas kernels  233 us (100%)
    pallas_call x1, Pallas kernels, on_device(): pl.pallas_call(functools.partial(kernel, n, m, LA, LW), out_shape=tuple((...  227 us
    pallas_call x1, Pallas kernels, on_device(): pl.pallas_call(put_kernel, out_shape=(jax.ShapeDtypeStruct((Z, 2, CH, R,...  5.95 us

profile of v4, /device:TPU:0, one launch (start us, length us, event | category | flops | bytes accessed | tf_op | source)
XLA Modules:
  0.0 233.3 jit_solution(5288799460339185092)
XLA Ops:
  0.6 226.7 %shard_map.143 = (bf16[4,2,40,8,2560]{4,3,2,1,0:T(8,128)(2,1)S(1)}, bf16[2560,1280]{1,0:T(8,128)(2,1)S(1)}, f32[40,8,2560]{2,1,0:T(8,128)S(1)}, bf16[1280]{0:T(1...) custom-call(f32[4,2,20,8,2560]{4,3,2,1,0:T(8,128)} %bitcast.13, ...), custom_call_target="tpu_custom_call" | custom-call | tf_op jit(solution)/shard_map/pallas_call | solution.py:788
  227.4 5.9 %shard_map.144 = (bf16[4,2,20,8,2560]{4,3,2,1,0:T(8,128)(2,1)}, bf16[2560,1280]{1,0:T(8,128)(2,1)}, bf16[1280]{0:T(1024)(128)(2,1)}, bf16[1280]{0:T(1024)(128)(2...) custom-call(bf16[4,2,40,8,2560]{4,3,2,1,0:T(8,128)(2,1)S(1)} %get-tuple-element.23.G, ...), custom_call_target="tpu_custom_call" | custom-call | tf_op jit(solution)/shard_map/pallas_call | solution.py:826

commit v5 on v4

--- a/solution.py
+++ b/solution.py
@@ -16,7 +16,8 @@
 HEAD, TAIL = 1, 1
 DEPTH = 4
 SENDS = 2
-LAST, LAST_SPLIT = 6, 0.75
+LAST, LAST_SPLIT = 8, 0.7
+FIRST, FIRST_SPLIT = 4, 0.7
 VMEM_BYTES = 66_000_000
 F32, BF16 = jnp.float32, jnp.bfloat16
 
@@ -26,6 +27,7 @@
     m,
     LA,
     LW,
+    LF,
     up_ref,
     down_ref,
     pup_ref,
@@ -49,6 +51,12 @@
     RYB,
     RZA,
     RZB,
+    XA1,
+    XB1,
+    RYA1,
+    RYB1,
+    RZA1,
+    RZB1,
     PR,
     SQ,
     V,
@@ -185,6 +193,27 @@
         free(copy, p)
         copy(p).start()
 
+    rest = (LA, XA, XB, RYA, RYB, RZA, RZB)
+    start = (LF, XA1, XB1, RYA1, RYB1, RZA1, RZB1)
+
+    def bufs(p, act):
+        @pl.when(p >= FIRST)
+        def _():
+            act(rest)
+
+        @pl.when(p < FIRST)
+        def _():
+            act(start)
+
+    def free_sum(copy, p):
+        @pl.when(p >= SENDS)
+        def _():
+            bufs(p - SENDS, lambda w: copy(p - SENDS, w).wait_send())
+
+    def go_sum(copy, p):
+        free_sum(copy, p)
+        bufs(p, lambda w: copy(p, w).start())
+
     def wide(p):
         return p >= C - LAST
 
@@ -284,13 +313,13 @@
 
     YA, YB, RA, LFA, RB, LFB, GYA, GYB, GRA, GLA, GRB, GLB = range(12)
 
-    def ya(p):
+    def ya(p, w):
         c = slot(p)
-        return remote(XA.at[c, 1 - y], RYA.at[c], YA, p, other)
-
-    def yb(p):
+        return remote(w[1].at[c, 1 - y], w[3].at[c], YA, p, other)
+
+    def yb(p, w):
         c = slot(p)
-        return remote(XB.at[c, z, 1 - y], RYB.at[c], YB, p, other)
+        return remote(w[2].at[c, z, 1 - y], w[4].at[c], YB, p, other)
 
     def gya(p, la):
         ref = G.at[:, y, slot(p), :, pl.ds(0, la)]
@@ -333,8 +362,8 @@
     def ya_piece(p, d):
         c = slot(p)
         return piece(
-            XA.at[c, 1 - y, d],
-            RYA.at[c, d],
+            XA1.at[c, 1 - y, d],
+            RYA1.at[c, d],
             send.at[YA, p % SENDS],
             first_recv.at[p, d],
             other,
@@ -343,16 +372,16 @@
     def take(p, d):
         c = slot(p)
         ya_piece(p, d).wait_recv()
-        XA[c, y, d] = (XA[c, y, d].astype(F32) + RYA[c, d].astype(F32)).astype(BF16)
+        XA1[c, y, d] = (XA1[c, y, d].astype(F32) + RYA1[c, d].astype(F32)).astype(BF16)
 
     inward = [d for i in range(Z // 2) for d in (Z - 1 - i, i)]
 
     def sum_piece(first, right, p, d):
         c = slot(p)
-        rz = RZA if first else RZB
+        rz = RZA1 if first else RZB1
         kind = (RA if first else RB) if right else (LFA if first else LFB)
         return piece(
-            XA.at[c, y, d] if first else XB.at[c, d],
+            XA1.at[c, y, d] if first else XB1.at[c, d],
             rz.at[c, d + 1 if right else d],
             send.at[kind, p % SENDS],
             sum_recv.at[2 * first + right, p, d],
@@ -378,43 +407,35 @@
         e = p - (C - TAIL)
         return piece(ref, ref, gather_send.at[e, d], gather_recv.at[4, e, d], other)
 
-    def x_ref(first, c):
-        return XA.at[c, y] if first else XB.at[c]
-
-    def sum_right(first, p, k):
+    def x_ref(first, c, w):
+        return w[1].at[c, y] if first else w[2].at[c]
+
+    def sum_right(first, p, k, w):
         c = slot(p)
-        rz = RZA if first else RZB
         return remote(
-            x_ref(first, c).at[pl.ds(k + 1, Z - 1 - k)],
-            rz.at[c, pl.ds(k + 2, Z - 1 - k)],
+            x_ref(first, c, w).at[pl.ds(k + 1, Z - 1 - k)],
+            w[5 if first else 6].at[c, pl.ds(k + 2, Z - 1 - k)],
             RA if first else RB,
             p,
             right_of(),
         )
 
-    def sum_left(first, p, k):
+    def sum_left(first, p, k, w):
         c = slot(p)
-        rz = RZA if first else RZB
         return remote(
-            x_ref(first, c).at[pl.ds(0, k)],
-            rz.at[c, pl.ds(0, k)],
+            x_ref(first, c, w).at[pl.ds(0, k)],
+            w[5 if first else 6].at[c, pl.ds(0, k)],
             LFA if first else LFB,
             p,
             left_of(),
         )
 
-    def add(first, p, lo, count, at):
+    def add(first, p, lo, count, at, w):
         c = slot(p)
-        rz = RZA if first else RZB
+        x, rz = (w[1], w[5]) if first else (w[2], w[6])
         for d in range(count):
-            if first:
-                XA[c, y, lo + d] = (
-                    XA[c, y, lo + d].astype(F32) + rz[c, at + d].astype(F32)
-                ).astype(BF16)
-            else:
-                XB[c, lo + d] = (
-                    XB[c, lo + d].astype(F32) + rz[c, at + d].astype(F32)
-                ).astype(BF16)
+            i = (c, y, lo + d) if first else (c, lo + d)
+            x[i] = (x[i].astype(F32) + rz[c, at + d].astype(F32)).astype(BF16)
 
     def at_hop(t, k, bulk, pieces, special):
         for right in (True, False):
@@ -432,35 +453,35 @@
     def reduce_step(first, t):
         for k in range(Z):
 
-            def to_right(p):
-                return sum_right(first, p, k)
-
-            def to_left(p):
-                return sum_left(first, p, k)
+            def to_right(p, w):
+                return sum_right(first, p, k, w)
+
+            def to_left(p, w):
+                return sum_left(first, p, k, w)
 
             def bulk(right, p):
-                if right:
-                    if k > 0:
-                        sum_right(first, p, k - 1).wait_recv()
-                        add(first, p, k, Z - k, k + 1)
-                    if k < Z - 1:
-                        go(to_right, p)
-                else:
-                    if k < Z - 1:
-                        sum_left(first, p, k + 1).wait_recv()
-                        add(first, p, 0, k + 1, 0)
-                    if k > 0:
-                        go(to_left, p)
+                def arrive(w):
+                    if right:
+                        sum_right(first, p, k - 1, w).wait_recv()
+                        add(first, p, k, Z - k, k + 1, w)
+                    else:
+                        sum_left(first, p, k + 1, w).wait_recv()
+                        add(first, p, 0, k + 1, 0, w)
+
+                if k > 0 if right else k < Z - 1:
+                    bufs(p, arrive)
+                if k < Z - 1 if right else k > 0:
+                    go_sum(to_right if right else to_left, p)
 
             def pieces(right, p):
                 if k < Z - 1 if right else k > 0:
-                    free(to_right if right else to_left, p)
+                    free_sum(to_right if right else to_left, p)
                 for d in range(Z - 1, k - 1, -1) if right else range(k + 1):
                     if first and k == (0 if right else Z - 1):
                         take(p, d)
                     if k > 0 if right else k < Z - 1:
                         sum_piece(first, right, p, d).wait_recv()
-                        add(first, p, d, 1, d + 1 if right else d)
+                        add(first, p, d, 1, d + 1 if right else d, start)
                     if d != k:
                         sum_piece(first, right, p, d).start()
 
@@ -516,7 +537,7 @@
             at_hop(t, k, bulk, pieces, tail)
 
     def last_sends(p):
-        for copy in (ya(p), yb(p), gyb(p, LW)):
+        for copy in (ya(p, rest), yb(p, rest), gyb(p, LW)):
             copy.wait_send()
         for o in range(1, m):
             sq_copy(p, o).wait_send()
@@ -526,10 +547,10 @@
             def _():
                 for first in (True, False):
                     if k < Z - 1:
-                        sum_right(first, p, k).wait_send()
+                        sum_right(first, p, k, rest).wait_send()
                         gather_right(first, p, k, LW).wait_send()
                     if k > 0:
-                        sum_left(first, p, k).wait_send()
+                        sum_left(first, p, k, rest).wait_send()
                         gather_left(first, p, k, LW).wait_send()
 
     def back_block(b):
@@ -572,20 +593,24 @@
 
         def cast(c):
             load_up(c).wait()
-            for d in range(Z):
-                for v in range(2):
-                    XA[c, v, d] = stage[c % 2, d, v, :, :LA].astype(BF16)
-                    XB[c, d, v] = stage[c % 2, d, v, :, LA:].astype(BF16)
+
+            def put(w):
+                for d in range(Z):
+                    for v in range(2):
+                        w[1][c, v, d] = stage[c % 2, d, v, :, : w[0]].astype(BF16)
+                        w[2][c, d, v] = stage[c % 2, d, v, :, w[0] :].astype(BF16)
+
+            bufs(t, put)
 
         load_at(t, cast)
 
         @pl.when((t < C) & jnp.logical_not(head(t)))
         def _():
-            go(ya, t)
+            go_sum(ya, t)
 
         @pl.when(head(t))
         def _():
-            free(ya, t)
+            free_sum(ya, t)
             for half in range(2):
 
                 @pl.when(z // (Z // 2) == half)
@@ -604,16 +629,22 @@
         @pl.when((s < C) & jnp.logical_not(head(s)))
         def _():
             c = slot(s)
-            ya(s).wait_recv()
-            for d in range(Z):
-                XA[c, y, d] = (XA[c, y, d].astype(F32) + RYA[c, d].astype(F32)).astype(BF16)
+
+            def arrive(w):
+                ya(s, w).wait_recv()
+                for d in range(Z):
+                    w[1][c, y, d] = (
+                        w[1][c, y, d].astype(F32) + w[3][c, d].astype(F32)
+                    ).astype(BF16)
+
+            bufs(s, arrive)
 
         reduce_step(True, s)
         b = t - (Z - 1)
 
         @when_chunk(b)
         def _():
-            go(yb, b)
+            go_sum(yb, b)
 
         u = t - Z
 
@@ -625,9 +656,14 @@
         @when_chunk(u)
         def _():
             f = slot(u)
-            yb(u).wait_recv()
-            NX[f, :, :LA] = XA[f, y, z].astype(F32) * rate
-            NX[f, :, LA:] = (XB[f, z, y].astype(F32) + RYB[f].astype(F32)) * rate
+
+            def arrive(w):
+                la = w[0]
+                yb(u, w).wait_recv()
+                NX[f, :, :la] = w[1][f, y, z].astype(F32) * rate
+                NX[f, :, la:] = (w[2][f, z, y].astype(F32) + w[4][f].astype(F32)) * rate
+
+            bufs(u, arrive)
             SQ[f, 0, 0] = lanes(NX[f])
             SQ[f, 0, 1] = lanes(PR[f])
             for o in range(1, m):
@@ -772,6 +808,7 @@
     C = 2 * CH
     LA = max(1, round(SPLIT * L / LANE)) * LANE
     LB = L - LA
+    LF = min(L // LANE - 1, round(FIRST_SPLIT * L / LANE)) * LANE
     LW = min(L // LANE - 1, round(LAST_SPLIT * L / LANE)) * LANE
     width = slope_norm.shape[1]
     up = slope_up[0].reshape(Z, 2, CH, R, L)
@@ -786,7 +823,7 @@
     kept += [((width,), BF16)] * 2 + [((rows,), F32)] * 2
     size = sum(jnp.dtype(dtype).itemsize * math.prod(shape) for shape, dtype in kept)
     held = pl.pallas_call(
-        functools.partial(kernel, n, m, LA, LW),
+        functools.partial(kernel, n, m, LA, LW, LF),
         out_shape=tuple(pltpu.VMEM(shape, dtype) for shape, dtype in kept),
         in_specs=[hbm] * 8,
         out_specs=(vmem,) * 7,
@@ -799,6 +836,12 @@
             pltpu.VMEM((C, R, LB), BF16),
             pltpu.VMEM((C, Z + 1, R, LA), BF16),
             pltpu.VMEM((C, Z + 1, 2, R, LB), BF16),
+            pltpu.VMEM((FIRST, 2, Z, R, LF), BF16),
+            pltpu.VMEM((FIRST, Z, 2, R, L - LF), BF16),
+            pltpu.VMEM((FIRST, Z, R, LF), BF16),
+            pltpu.VMEM((FIRST, R, L - LF), BF16),
+            pltpu.VMEM((FIRST, Z + 1, R, LF), BF16),
+            pltpu.VMEM((FIRST, Z + 1, 2, R, L - LF), BF16),
             pltpu.VMEM((C, R, L), F32),
             pltpu.VMEM((C, m, 2, R, LANE), F32),
             pltpu.VMEM((2, 1, width), F32),
@@ -809,13 +852,13 @@
             pltpu.SemaphoreType.DMA((DEPTH,)),
             pltpu.SemaphoreType.DMA((6,)),
             pltpu.SemaphoreType.DMA((12, SENDS)),
-            pltpu.SemaphoreType.DMA((12, Z + 2)),
+            pltpu.SemaphoreType.DMA((12, Z + 1)),
             pltpu.SemaphoreType.DMA((HEAD, Z)),
             pltpu.SemaphoreType.DMA((4, HEAD, Z)),
             pltpu.SemaphoreType.DMA((5, TAIL, Z)),
             pltpu.SemaphoreType.DMA((TAIL, Z)),
             pltpu.SemaphoreType.DMA((m - 1, SENDS)),
-            pltpu.SemaphoreType.DMA((m - 1, Z + 2)),
+            pltpu.SemaphoreType.DMA((m - 1, Z + 1)),
             pltpu.SemaphoreType.DMA((3,)),
             pltpu.SemaphoreType.DMA((3,)),
         ],

time: 233 us -> 232 us (level)
  no operation moved by 1% of the time
where the time goes in v5:
time: 232 us
  Pallas kernels  232 us (100%)
    pallas_call x1, Pallas kernels, on_device(): pl.pallas_call(functools.partial(kernel, n, m, LA, LW, LF), out_shape=tup...  226 us
    pallas_call x1, Pallas kernels, on_device(): pl.pallas_call(put_kernel, out_shape=(jax.ShapeDtypeStruct((Z, 2, CH, R,...  5.95 us

profile of v5, /device:TPU:0, one launch (start us, length us, event | category | flops | bytes accessed | tf_op | source)
XLA Modules:
  0.0 232.3 jit_solution(4621622241351051475)
XLA Ops:
  0.6 225.7 %shard_map.143 = (bf16[4,2,40,8,2560]{4,3,2,1,0:T(8,128)(2,1)S(1)}, bf16[2560,1280]{1,0:T(8,128)(2,1)S(1)}, f32[40,8,2560]{2,1,0:T(8,128)S(1)}, bf16[1280]{0:T(1...) custom-call(f32[4,2,20,8,2560]{4,3,2,1,0:T(8,128)} %bitcast.13, ...), custom_call_target="tpu_custom_call" | custom-call | tf_op jit(solution)/shard_map/pallas_call | solution.py:825
  226.3 5.9 %shard_map.144 = (bf16[4,2,20,8,2560]{4,3,2,1,0:T(8,128)(2,1)}, bf16[2560,1280]{1,0:T(8,128)(2,1)}, bf16[1280]{0:T(1024)(128)(2,1)}, bf16[1280]{0:T(1024)(128)(2...) custom-call(bf16[4,2,40,8,2560]{4,3,2,1,0:T(8,128)(2,1)S(1)} %get-tuple-element.23.G, ...), custom_call_target="tpu_custom_call" | custom-call | tf_op jit(solution)/shard_map/pallas_call | solution.py:869

commit v6 on v5

--- a/solution.py
+++ b/solution.py
@@ -146,11 +146,6 @@
         ]
 
     load_up(0).start()
-    for d in load_params() + load_vectors():
-        d.start()
-
-    for b in range(min(DEPTH - 1, blocks)):
-        load_down(b).start()
 
     barrier = pltpu.get_barrier_semaphore()
     def greet(to):
@@ -620,6 +615,16 @@
 
         reduce_step(False, t)
         s = t - 1
+
+        @pl.when(t == 0)
+        def _():
+            for d in load_vectors():
+                d.start()
+            for b in range(min(DEPTH - 1, blocks)):
+                load_down(b).start()
+            for d in load_params():
+                d.start()
+
 
         @pl.when((s >= 0) & head(s) & (z > 0) & (z < Z - 1))
         def _():

time: 232 us -> 231 us (level)
  no operation moved by 1% of the time
where the time goes in v6:
time: 231 us
  Pallas kernels  230 us (100%)
    pallas_call x1, Pallas kernels, on_device(): pl.pallas_call(functools.partial(kernel, n, m, LA, LW, LF), out_shape=tup...  224 us
    pallas_call x1, Pallas kernels, on_device(): pl.pallas_call(put_kernel, out_shape=(jax.ShapeDtypeStruct((Z, 2, CH, R,...  5.95 us

profile of v6, /device:TPU:0, one launch (start us, length us, event | category | flops | bytes accessed | tf_op | source)
XLA Modules:
  0.0 230.9 jit_solution(4726900830870198237)
XLA Ops:
  0.6 224.3 %shard_map.143 = (bf16[4,2,40,8,2560]{4,3,2,1,0:T(8,128)(2,1)S(1)}, bf16[2560,1280]{1,0:T(8,128)(2,1)S(1)}, f32[40,8,2560]{2,1,0:T(8,128)S(1)}, bf16[1280]{0:T(1...) custom-call(f32[4,2,20,8,2560]{4,3,2,1,0:T(8,128)} %bitcast.13, ...), custom_call_target="tpu_custom_call" | custom-call | tf_op jit(solution)/shard_map/pallas_call | solution.py:830
  224.9 5.9 %shard_map.144 = (bf16[4,2,20,8,2560]{4,3,2,1,0:T(8,128)(2,1)}, bf16[2560,1280]{1,0:T(8,128)(2,1)}, bf16[1280]{0:T(1024)(128)(2,1)}, bf16[1280]{0:T(1024)(128)(2...) custom-call(bf16[4,2,40,8,2560]{4,3,2,1,0:T(8,128)(2,1)S(1)} %get-tuple-element.23.G, ...), custom_call_target="tpu_custom_call" | custom-call | tf_op jit(solution)/shard_map/pallas_call | solution.py:874
